TPU v7x, 8 devices: a whole 2x2x1 slice. The times are simulated.
8 devices in a mesh: dp: 1 (over z), tp: 2 (over y), cp: 4 (over x, core).
Axes of the slice: x: 2, y: 2, z: 1, core: 2. Of those that a mesh axis runs over, the one named last changes fastest.
Arguments:
- hidden: bfloat16 [4096, 2560], P(('dp', 'cp'))
- start_pos: int32 [1], P('dp')
- k_local: bfloat16 [1024, 4, 256], P('dp', 'tp')
- v_local: bfloat16 [1024, 4, 256], P('dp', 'tp')
- k_global: bfloat16 [24576, 4, 256], P(('dp', 'cp'), 'tp')
- v_global: bfloat16 [24576, 4, 256], P(('dp', 'cp'), 'tp')
- w_query: bfloat16 [2, 2560, 2048], P(None, None, 'tp')
- w_key: bfloat16 [2, 2560, 1024], P(None, None, 'tp')
- w_value: bfloat16 [2, 2560, 1024], P(None, None, 'tp')
- w_out: bfloat16 [2, 2048, 2560], P(None, 'tp')
- w_gate: bfloat16 [2, 2560, 10240], P(None, None, 'tp')
- w_up: bfloat16 [2, 2560, 10240], P(None, None, 'tp')
- w_down: bfloat16 [2, 10240, 2560], P(None, 'tp')
- norm_gain: float32 [2, 4, 2560], replicated
- qk_gain: float32 [2, 2, 256], replicated
Outputs:
- output 1: bfloat16 [4096, 2560], P(('dp', 'cp'))
- output 2: bfloat16 [4096, 4, 256], P(('dp', 'cp'), 'tp')
- output 3: bfloat16 [4096, 4, 256], P(('dp', 'cp'), 'tp')
- output 4: bfloat16 [4096, 4, 256], P(('dp', 'cp'), 'tp')
- output 5: bfloat16 [4096, 4, 256], P(('dp', 'cp'), 'tp')
All inputs are finite; a program needn't handle non-finite values.
Results may differ from a plain program's by a relative error of at most 0.0198273.
Values are sent between devices in bfloat16 or wider.
A program may use at most 1 GiB of HBM per device.

v0:
```python
import jax
import jax.numpy as jnp
from jax import lax
from jax.sharding import PartitionSpec as P

NORM_EPS = 1e-6
LOCAL_BASE = 10000.0
GLOBAL_BASE = 1000000.0
GLOBAL_DIV = 8.0
NEG_BIG = -1e30


def rms_scale(values, gain_vec):
    return values * lax.rsqrt(jnp.mean(values * values, axis=-1, keepdims=True) + NORM_EPS) * (1.0 + gain_vec)


def rotate(values, positions, rope_base, divisor):
    half_dim = values.shape[-1] // 2
    inv_freq = 1.0 / (rope_base ** (jnp.arange(0, 2 * half_dim, 2, dtype=jnp.float32) / (2 * half_dim)))
    angles = (positions.astype(jnp.float32) / divisor)[:, None] * inv_freq[None, :]
    angles = jnp.concatenate([angles, angles], axis=-1)[:, None, :]
    turned = jnp.concatenate([-values[..., half_dim:], values[..., :half_dim]], axis=-1)
    return values * jnp.cos(angles) + turned * jnp.sin(angles)


def project(hidden, layer_gains, qk_pair, w_query, w_key, w_value, positions, rope_base, divisor):
    row_count = hidden.shape[0]
    head_dim = qk_pair.shape[-1]
    normed = rms_scale(hidden.astype(jnp.float32), layer_gains[0]).astype(jnp.bfloat16)
    queries = jnp.dot(normed, w_query, preferred_element_type=jnp.float32).reshape(row_count, -1, head_dim)
    key_new = jnp.dot(normed, w_key, preferred_element_type=jnp.float32).reshape(row_count, -1, head_dim)
    value_new = jnp.dot(normed, w_value, preferred_element_type=jnp.float32).astype(jnp.bfloat16).reshape(row_count, -1, head_dim)
    queries = rotate(rms_scale(queries, qk_pair[0]), positions, rope_base, divisor).astype(jnp.bfloat16)
    key_new = rotate(rms_scale(key_new, qk_pair[1]), positions, rope_base, divisor).astype(jnp.bfloat16)
    return queries.reshape(row_count, key_new.shape[1], -1, head_dim), key_new, value_new


def finish(hidden, attn_out, layer_gains, w_out, w_gate, w_up, w_down):
    row_count = hidden.shape[0]
    attn_proj = lax.psum(jnp.dot(attn_out.reshape(row_count, -1), w_out, preferred_element_type=jnp.float32).astype(jnp.bfloat16), 'tp')
    residual = (hidden.astype(jnp.float32) + rms_scale(attn_proj.astype(jnp.float32), layer_gains[1])).astype(jnp.bfloat16)
    normed = rms_scale(residual.astype(jnp.float32), layer_gains[2]).astype(jnp.bfloat16)
    gate_proj = jnp.dot(normed, w_gate, preferred_element_type=jnp.float32)
    up_proj = jnp.dot(normed, w_up, preferred_element_type=jnp.float32)
    hidden_act = (jax.nn.gelu(gate_proj, approximate=True) * up_proj).astype(jnp.bfloat16)
    down_proj = lax.psum(jnp.dot(hidden_act, w_down, preferred_element_type=jnp.float32).astype(jnp.bfloat16), 'tp')
    return (residual.astype(jnp.float32) + rms_scale(down_proj.astype(jnp.float32), layer_gains[3])).astype(jnp.bfloat16)


def window_attention(queries, key_new, value_new, k_cache, v_cache, first_pos, positions, cp_index, cp_size):
    row_count = queries.shape[0]
    window = k_cache.shape[0]
    tail_len = min(window, row_count)
    step_count = min(cp_size - 1, -(-window // row_count))
    key_parts = [k_cache]
    value_parts = [v_cache]
    pos_parts = [first_pos - window + jnp.remainder(jnp.arange(window) - first_pos, window)]
    ok_parts = [jnp.ones((window,), dtype=bool)]
    for step_back in range(step_count, 0, -1):
        sender_pairs = [(sender, sender + step_back) for sender in range(cp_size - step_back)]
        got_key, got_value = lax.ppermute((key_new[row_count - tail_len:], value_new[row_count - tail_len:]), 'cp', sender_pairs)
        key_parts.append(got_key)
        value_parts.append(got_value)
        pos_parts.append(positions[row_count - tail_len:] - step_back * row_count)
        ok_parts.append(jnp.broadcast_to(cp_index >= step_back, (tail_len,)))
    key_parts.append(key_new)
    value_parts.append(value_new)
    pos_parts.append(positions)
    ok_parts.append(jnp.ones((row_count,), dtype=bool))
    key_all = jnp.concatenate(key_parts, axis=0)
    value_all = jnp.concatenate(value_parts, axis=0)
    key_pos = jnp.concatenate(pos_parts)
    key_ok = jnp.concatenate(ok_parts)
    distance = positions[:, None] - key_pos[None, :]
    visible = key_ok[None, :] & (distance >= 0) & (distance < window)
    scores = jnp.einsum('qkgd,tkd->qkgt', queries, key_all, preferred_element_type=jnp.float32) * queries.shape[-1] ** -0.5
    scores = jnp.where(visible[:, None, None, :], scores, NEG_BIG)
    attn_prob = jax.nn.softmax(scores, axis=-1).astype(jnp.bfloat16)
    return jnp.einsum('qkgt,tkd->qkgd', attn_prob, value_all, preferred_element_type=jnp.float32).astype(jnp.bfloat16)


def partial_block(block_q, query_rel, cache_k, cache_v, cache_ok, own_k, own_v, own_rel):
    scale = block_q.shape[-1] ** -0.5
    cache_scores = jnp.einsum('qkgd,tkd->qkgt', block_q, cache_k, preferred_element_type=jnp.float32) * scale
    cache_scores = jnp.where(cache_ok[None, None, None, :], cache_scores, NEG_BIG)
    own_scores = jnp.einsum('qkgd,tkd->qkgt', block_q, own_k, preferred_element_type=jnp.float32) * scale
    own_seen = own_rel[None, :] <= query_rel[:, None]
    own_scores = jnp.where(own_seen[:, None, None, :], own_scores, NEG_BIG)
    row_max = jnp.maximum(cache_scores.max(axis=-1), own_scores.max(axis=-1))
    cache_exp = jnp.exp(cache_scores - row_max[..., None])
    own_exp = jnp.exp(own_scores - row_max[..., None])
    row_sum = cache_exp.sum(axis=-1) + own_exp.sum(axis=-1)
    weighted = jnp.einsum('qkgt,tkd->qkgd', cache_exp.astype(jnp.bfloat16), cache_v, preferred_element_type=jnp.float32)
    weighted = weighted + jnp.einsum('qkgt,tkd->qkgd', own_exp.astype(jnp.bfloat16), own_v, preferred_element_type=jnp.float32)
    return weighted, jnp.stack([row_max, row_sum], axis=-1)


def merge_parts(part_out, part_stats):
    best_max = part_stats[..., 0].max(axis=0)
    factors = jnp.exp(part_stats[..., 0] - best_max)
    norm_sum = (factors * part_stats[..., 1]).sum(axis=0)
    weighted = (part_out * factors[..., None]).sum(axis=0)
    return (weighted / norm_sum[..., None]).astype(jnp.bfloat16)


def spread_attention(queries, key_new, value_new, k_cache, v_cache, first_pos, cp_index, cp_size):
    row_count = queries.shape[0]
    shard_len = k_cache.shape[0]
    all_queries = lax.all_gather(queries, 'cp')
    cache_ok = (cp_index * shard_len + jnp.arange(shard_len)) < first_pos
    own_rel = cp_index * row_count + jnp.arange(row_count)

    def one_block(block_args):
        block_q, block_index = block_args
        query_rel = block_index * row_count + jnp.arange(row_count)
        return partial_block(block_q, query_rel, k_cache, v_cache, cache_ok, key_new, value_new, own_rel)

    part_out, part_stats = lax.map(one_block, (all_queries, jnp.arange(cp_size)))
    got_out = lax.all_to_all(part_out, 'cp', 0, 0, tiled=True)
    got_stats = lax.all_to_all(part_stats, 'cp', 0, 0, tiled=True)
    return merge_parts(got_out, got_stats)


def solution(mesh):
    cp_size = mesh.shape['cp']
    row_spec = P(('dp', 'cp'), None)
    cache_spec = P(('dp', 'cp'), 'tp', None)
    window_spec = P('dp', 'tp', None)
    col_spec = P(None, None, 'tp')
    row_split = P(None, 'tp', None)
    replicated = P()

    def device_step(hidden, start_pos, k_local, v_local, k_global, v_global, w_query, w_key, w_value, w_out, w_gate, w_up, w_down, norm_gain, qk_gain):
        first_pos = start_pos[0]
        cp_index = lax.axis_index('cp')
        row_count = hidden.shape[0]
        positions = first_pos + cp_index * row_count + jnp.arange(row_count)
        queries, key_loc, value_loc = project(hidden, norm_gain[0], qk_gain[0], w_query[0], w_key[0], w_value[0], positions, LOCAL_BASE, 1.0)
        attn_out = window_attention(queries, key_loc, value_loc, k_local, v_local, first_pos, positions, cp_index, cp_size)
        middle = finish(hidden, attn_out, norm_gain[0], w_out[0], w_gate[0], w_up[0], w_down[0])
        queries, key_glob, value_glob = project(middle, norm_gain[1], qk_gain[1], w_query[1], w_key[1], w_value[1], positions, GLOBAL_BASE, GLOBAL_DIV)
        attn_out = spread_attention(queries, key_glob, value_glob, k_global, v_global, first_pos, cp_index, cp_size)
        final_out = finish(middle, attn_out, norm_gain[1], w_out[1], w_gate[1], w_up[1], w_down[1])
        return final_out, key_loc, value_loc, key_glob, value_glob

    return jax.shard_map(device_step, mesh=mesh, in_specs=(row_spec, P('dp'), window_spec, window_spec, cache_spec, cache_spec, col_spec, col_spec, col_spec, row_split, col_spec, col_spec, row_split, replicated, replicated), out_specs=(row_spec, cache_spec, cache_spec, cache_spec, cache_spec), check_vma=False)
```

profile of v0, /device:TPU:0, one launch (start us, length us, event | category | flops | bytes accessed | tf_op | source)
XLA Modules:
  0.0 1770.9 jit_solution(3996112366884865355)
XLA Ops:
  155.7 124.7 %all-reduce.5.cloned.1.call-done = bf16[1024,2560]{1,0:T(8,128)(2,1)} async-done(((bf16[1024,2560]{1,0:T(8,128)(2,1)}), bf16[1024,2560]{1,0:T(8,128)(2,1)}) %all-reduce.5.cloned.1.call-update) | async-done | bytes 5242896 | tf_op jit(solution)/shard_map/psum | solution.py:40
  291.9 32.7 %fusion.52 = f32[1024,5120]{1,0:T(8,128)} fusion(bf16[2,2560,5120]{2,1,0:T(8,128)(2,1)} %param.27, bf16[1024,2560]{1,0:T(8,128)(2,1)S(1)} %get-tuple-element.183, f32[2560]{0:T(1024)S(1)} %copy-done.26, f32[1024]{0:T(1024)S(1)} %add_rsqrt_fusion.9), kind=kOutput, calls=%fused_computation.62 | convolution fusion | flops 26854031360 | bytes 52443136 | tf_op jit(solution)/shard_map/dot_general | solution.py:43
  324.6 38.2 %fusion.72.clone.7 = bf16[1024,5120]{1,0:T(8,128)(2,1)} fusion(f32[1024,5120]{1,0:T(8,128)} %fusion.52, bf16[2,2560,5120]{2,1,0:T(8,128)(2,1)} %param.28, bf16[1024,2560]{1,0:T(8,128)(2,1)} %copy-done.1, f32[2560]{0:T(1024)S(1)} %copy-done.26, f32[1024]{0:T(1024)S(1)} %add_rsqrt_fusion.9), kind=kOutput, calls=%fused_computation.82.clone.clone.clone.clone.clone.2 | convolution fusion | flops 26906460160 | bytes 62928896 | tf_op jit(solution)/shard_map/dot_general | solution.py:44
  362.9 34.7 %fusion.124 = bf16[1024,2560]{1,0:T(8,128)(2,1)} fusion(bf16[2,5120,2560]{2,1,0:T(8,128)(2,1)} %param.29, bf16[1024,5120]{1,0:T(8,128)(2,1)} %fusion.72.clone.7), kind=kOutput, calls=%fused_computation.149 | convolution fusion | flops 26846167040 | bytes 41943040 | tf_op jit(solution)/shard_map/dot_general | solution.py:46
  409.4 113.0 %all-reduce.7.cloned.1.call-done = bf16[1024,2560]{1,0:T(8,128)(2,1)} async-done(((bf16[1024,2560]{1,0:T(8,128)(2,1)}), bf16[1024,2560]{1,0:T(8,128)(2,1)}) %all-reduce.7.cloned.1.call-update) | async-done | bytes 5242896 | tf_op jit(solution)/shard_map/psum | solution.py:46
  605.4 562.5 %while.13 = (s32[]{:T(128)}, f32[4,1024,2,2,256]{4,1,3,2,0:T(8,128)}, f32[4,1024,2,2,2]{1,3,2,4,0:T(2,128)S(1)}, bf16[4,1024,2,2,256]{4,1,3,2,0:T(8,128)(2,1)}, ...) while((s32[]{:T(128)}, ...), condition=%wide.region_18.19_spmd.clone, body=%wide.region_13.18_spmd.clone.sunk | while | flops 30389843968 | bytes 388310720 | solution.py:118
  617.0 38.0 %bitcast_reduce_fusion.6 = (f32[1024,2,2]{0,2,1:T(2,128)S(1)}, f32[2,1024,2,6144]{3,1,2,0:T(8,128)}) fusion(pred[6144]{0:T(1024)(128)(4,1)S(1)} %add_compare_fusion.2, bf16[6144,2,256]{2,0,1:T(8,128)(2,1)} %get-tuple-element.339, bf16[4,1024,2,2,256]{4,1,3,2,0:T(8,128)(2,1)} %get-tuple-element.338, s32[]{:T(128)} %get-tuple-element.321), kind=kOutput, calls=%fused_computation.3.clone.1 | convolution fusion | flops 12960395264 | bytes 109074944 | tf_op jit(solution)/shard_map/while/body/eval_jaxpr/qkgd,tkd->qkgt/dot_general | solution.py:84
  655.1 31.3 %fusion.268 = f32[1024,2,2]{0,2,1:T(2,128)S(1)} fusion(f32[2,1024,2,6144]{3,1,2,0:T(8,128)} %get-tuple-element.306, f32[1024,2,2]{0,2,1:T(2,128)S(1)} %max.19, pred[6144]{0:T(1024)(128)(4,1)S(1)} %add_compare_fusion.2), kind=kLoop, calls=%fused_computation.6.clone.1 | loop fusion | flops 100659200 | bytes 100702208 | tf_op jit(solution)/shard_map/while/body/eval_jaxpr/reduce_sum | solution.py:92
  707.3 38.8 %bitcast_dynamic-update-slice_fusion.2 = f32[4,1024,2,2,256]{4,1,3,2,0:T(8,128)} fusion(f32[4,1024,2,2,256]{4,1,3,2,0:T(8,128)} %get-tuple-element.322, s32[]{:T(128)} %get-tuple-element.321, f32[2,1024,2,256]{3,1,2,0:T(8,128)} %fusion.267, bf16[6144,2,256]{2,0,1:T(8,128)(2,1)} %get-tuple-element.342, f32[2,1024,2,6144]{3,1,2,0:T(8,128)} %get-tuple-element.306, ...), kind=kOutput, calls=%fused_computation.24.clone.1 | convolution fusion | flops 12986613760 | bytes 115366400 | tf_op jit(solution)/shard_map/while/body/eval_jaxpr/qkgt,tkd->qkgd/dot_general | solution.py:93
  757.6 38.0 %bitcast_reduce_fusion.6 = (f32[1024,2,2]{0,2,1:T(2,128)S(1)}, f32[2,1024,2,6144]{3,1,2,0:T(8,128)}) fusion(pred[6144]{0:T(1024)(128)(4,1)S(1)} %add_compare_fusion.2, bf16[6144,2,256]{2,0,1:T(8,128)(2,1)} %get-tuple-element.339, bf16[4,1024,2,2,256]{4,1,3,2,0:T(8,128)(2,1)} %get-tuple-element.338, s32[]{:T(128)} %get-tuple-element.321), kind=kOutput, calls=%fused_computation.3.clone.1 | convolution fusion | flops 12960395264 | bytes 109074944 | tf_op jit(solution)/shard_map/while/body/eval_jaxpr/qkgd,tkd->qkgt/dot_general | solution.py:84
  795.6 31.3 %fusion.268 = f32[1024,2,2]{0,2,1:T(2,128)S(1)} fusion(f32[2,1024,2,6144]{3,1,2,0:T(8,128)} %get-tuple-element.306, f32[1024,2,2]{0,2,1:T(2,128)S(1)} %max.19, pred[6144]{0:T(1024)(128)(4,1)S(1)} %add_compare_fusion.2), kind=kLoop, calls=%fused_computation.6.clone.1 | loop fusion | flops 100659200 | bytes 100702208 | tf_op jit(solution)/shard_map/while/body/eval_jaxpr/reduce_sum | solution.py:92
  847.8 38.8 %bitcast_dynamic-update-slice_fusion.2 = f32[4,1024,2,2,256]{4,1,3,2,0:T(8,128)} fusion(f32[4,1024,2,2,256]{4,1,3,2,0:T(8,128)} %get-tuple-element.322, s32[]{:T(128)} %get-tuple-element.321, f32[2,1024,2,256]{3,1,2,0:T(8,128)} %fusion.267, bf16[6144,2,256]{2,0,1:T(8,128)(2,1)} %get-tuple-element.342, f32[2,1024,2,6144]{3,1,2,0:T(8,128)} %get-tuple-element.306, ...), kind=kOutput, calls=%fused_computation.24.clone.1 | convolution fusion | flops 12986613760 | bytes 115366400 | tf_op jit(solution)/shard_map/while/body/eval_jaxpr/qkgt,tkd->qkgd/dot_general | solution.py:93
  898.1 38.0 %bitcast_reduce_fusion.6 = (f32[1024,2,2]{0,2,1:T(2,128)S(1)}, f32[2,1024,2,6144]{3,1,2,0:T(8,128)}) fusion(pred[6144]{0:T(1024)(128)(4,1)S(1)} %add_compare_fusion.2, bf16[6144,2,256]{2,0,1:T(8,128)(2,1)} %get-tuple-element.339, bf16[4,1024,2,2,256]{4,1,3,2,0:T(8,128)(2,1)} %get-tuple-element.338, s32[]{:T(128)} %get-tuple-element.321), kind=kOutput, calls=%fused_computation.3.clone.1 | convolution fusion | flops 12960395264 | bytes 109074944 | tf_op jit(solution)/shard_map/while/body/eval_jaxpr/qkgd,tkd->qkgt/dot_general | solution.py:84
  936.1 31.3 %fusion.268 = f32[1024,2,2]{0,2,1:T(2,128)S(1)} fusion(f32[2,1024,2,6144]{3,1,2,0:T(8,128)} %get-tuple-element.306, f32[1024,2,2]{0,2,1:T(2,128)S(1)} %max.19, pred[6144]{0:T(1024)(128)(4,1)S(1)} %add_compare_fusion.2), kind=kLoop, calls=%fused_computation.6.clone.1 | loop fusion | flops 100659200 | bytes 100702208 | tf_op jit(solution)/shard_map/while/body/eval_jaxpr/reduce_sum | solution.py:92
  988.3 38.8 %bitcast_dynamic-update-slice_fusion.2 = f32[4,1024,2,2,256]{4,1,3,2,0:T(8,128)} fusion(f32[4,1024,2,2,256]{4,1,3,2,0:T(8,128)} %get-tuple-element.322, s32[]{:T(128)} %get-tuple-element.321, f32[2,1024,2,256]{3,1,2,0:T(8,128)} %fusion.267, bf16[6144,2,256]{2,0,1:T(8,128)(2,1)} %get-tuple-element.342, f32[2,1024,2,6144]{3,1,2,0:T(8,128)} %get-tuple-element.306, ...), kind=kOutput, calls=%fused_computation.24.clone.1 | convolution fusion | flops 12986613760 | bytes 115366400 | tf_op jit(solution)/shard_map/while/body/eval_jaxpr/qkgt,tkd->qkgd/dot_general | solution.py:93
  1038.6 38.0 %bitcast_reduce_fusion.6 = (f32[1024,2,2]{0,2,1:T(2,128)S(1)}, f32[2,1024,2,6144]{3,1,2,0:T(8,128)}) fusion(pred[6144]{0:T(1024)(128)(4,1)S(1)} %add_compare_fusion.2, bf16[6144,2,256]{2,0,1:T(8,128)(2,1)} %get-tuple-element.339, bf16[4,1024,2,2,256]{4,1,3,2,0:T(8,128)(2,1)} %get-tuple-element.338, s32[]{:T(128)} %get-tuple-element.321), kind=kOutput, calls=%fused_computation.3.clone.1 | convolution fusion | flops 12960395264 | bytes 109074944 | tf_op jit(solution)/shard_map/while/body/eval_jaxpr/qkgd,tkd->qkgt/dot_general | solution.py:84
  1076.7 31.3 %fusion.268 = f32[1024,2,2]{0,2,1:T(2,128)S(1)} fusion(f32[2,1024,2,6144]{3,1,2,0:T(8,128)} %get-tuple-element.306, f32[1024,2,2]{0,2,1:T(2,128)S(1)} %max.19, pred[6144]{0:T(1024)(128)(4,1)S(1)} %add_compare_fusion.2), kind=kLoop, calls=%fused_computation.6.clone.1 | loop fusion | flops 100659200 | bytes 100702208 | tf_op jit(solution)/shard_map/while/body/eval_jaxpr/reduce_sum | solution.py:92
  1128.9 38.8 %bitcast_dynamic-update-slice_fusion.2 = f32[4,1024,2,2,256]{4,1,3,2,0:T(8,128)} fusion(f32[4,1024,2,2,256]{4,1,3,2,0:T(8,128)} %get-tuple-element.322, s32[]{:T(128)} %get-tuple-element.321, f32[2,1024,2,256]{3,1,2,0:T(8,128)} %fusion.267, bf16[6144,2,256]{2,0,1:T(8,128)(2,1)} %get-tuple-element.342, f32[2,1024,2,6144]{3,1,2,0:T(8,128)} %get-tuple-element.306, ...), kind=kOutput, calls=%fused_computation.24.clone.1 | convolution fusion | flops 12986613760 | bytes 115366400 | tf_op jit(solution)/shard_map/while/body/eval_jaxpr/qkgt,tkd->qkgd/dot_general | solution.py:93
  1182.1 182.5 %all-to-all-done = f32[4,1024,2,2,256]{4,1,3,2,0:T(8,128)} async-done(((f32[4,1024,2,2,256]{4,1,3,2,0:T(8,128)}), f32[4,1024,2,2,256]{4,1,3,2,0:T(8,128)}, u32[]{:S(2)}, u32[]{:S(2)}) %all-to-all-start) | async-done | bytes 16777248 | tf_op jit(solution)/shard_map/all_to_all | solution.py:119
  1385.6 124.8 %all-reduce.9.cloned.1.call-done = bf16[1024,2560]{1,0:T(8,128)(2,1)} async-done(((bf16[1024,2560]{1,0:T(8,128)(2,1)}), bf16[1024,2560]{1,0:T(8,128)(2,1)}) %all-reduce.9.cloned.1.call-update) | async-done | bytes 5242896 | tf_op jit(solution)/shard_map/psum | solution.py:40
  1522.0 33.0 %fusion.46 = f32[1024,5120]{1,0:T(8,128)} fusion(bf16[2,2560,5120]{2,1,0:T(8,128)(2,1)} %param.27, bf16[1024,2560]{1,0:T(8,128)(2,1)S(1)} %get-tuple-element.179, f32[2560]{0:T(1024)S(1)} %copy-done.24, f32[1024]{0:T(1024)S(1)} %add_rsqrt_fusion.5), kind=kOutput, calls=%fused_computation.56 | convolution fusion | flops 26854031360 | bytes 52443136 | tf_op jit(solution)/shard_map/dot_general | solution.py:43
  1555.0 38.3 %fusion.81.clone.7 = bf16[1024,5120]{1,0:T(8,128)(2,1)} fusion(f32[1024,5120]{1,0:T(8,128)} %fusion.46, bf16[2,2560,5120]{2,1,0:T(8,128)(2,1)} %param.28, bf16[1024,2560]{1,0:T(8,128)(2,1)} %copy-done.2, f32[2560]{0:T(1024)S(1)} %copy-done.24, f32[1024]{0:T(1024)S(1)} %add_rsqrt_fusion.5), kind=kOutput, calls=%fused_computation.91.clone.clone.clone.clone.clone.2 | convolution fusion | flops 26906460160 | bytes 62928896 | tf_op jit(solution)/shard_map/dot_general | solution.py:44
  1593.3 34.7 %fusion.129 = bf16[1024,2560]{1,0:T(8,128)(2,1)} fusion(bf16[2,5120,2560]{2,1,0:T(8,128)(2,1)} %param.29, bf16[1024,5120]{1,0:T(8,128)(2,1)} %fusion.81.clone.7), kind=kOutput, calls=%fused_computation.150 | convolution fusion | flops 26846167040 | bytes 41943040 | tf_op jit(solution)/shard_map/dot_general | solution.py:46
  1639.6 113.3 %all-reduce.11.cloned.1.call-done = bf16[1024,2560]{1,0:T(8,128)(2,1)} async-done(((bf16[1024,2560]{1,0:T(8,128)(2,1)}), bf16[1024,2560]{1,0:T(8,128)(2,1)}) %all-reduce.11.cloned.1.call-update) | async-done | bytes 5242896 | tf_op jit(solution)/shard_map/psum | solution.py:46
  (208 shorter events, 450.0 us)
Async XLA Ops:
  7.2 273.3 %all-reduce.5.cloned.1.call-start = ((), (), s32[]{:S(2)}) async-start(), calls=%async_computation.2 | async-start | bytes 10485760 | tf_op jit(solution)/shard_map/psum | solution.py:40
  25.2 13.8 slice-start
  27.4 11.5 slice-start.1
  35.2 63.1 %collective-permute-start.1 = (bf16[1024,2,256]{0,2,1:T(8,128)(2,1)}, bf16[1024,2,256]{0,2,1:T(8,128)(2,1)}, u32[]{:S(2)}, u32[]{:S(2)}) collective-permute-start(bf16[1024,2,256]{0,2,1:T(8,128)(2,1)} %fusion.163), channel_id=1, source_target_pairs={{0,1},{1,2},{2,3},{4,5},{5,6},{6,7}} | collective-permute-start | bytes 3145736 | tf_op jit(solution)/shard_map/ppermute | solution.py:61
  44.7 81.5 %collective-permute-start = (bf16[1024,2,256]{0,2,1:T(8,128)(2,1)}, bf16[1024,2,256]{0,2,1:T(8,128)(2,1)}, u32[]{:S(2)}, u32[]{:S(2)}) collective-permute-start(bf16[1024,2,256]{0,2,1:T(8,128)(2,1)} %bitcast.1), channel_id=1, source_target_pairs={{0,1},{1,2},{2,3},{4,5},{5,6},{6,7}} | collective-permute-start | bytes 3145736 | tf_op jit(solution)/shard_map/ppermute | solution.py:61
  155.5 128.7 %copy-start.23 = (f32[2560]{0:T(1024)S(1)}, f32[2560]{0:T(1024)}, u32[]{:S(2)}) copy-start(f32[2560]{0:T(1024)} %get-tuple-element.151) | copy-start | bytes 30724
  155.5 367.0 %all-reduce.7.cloned.1.call-start = ((), (), s32[]{:S(2)}) async-start(), calls=%async_computation.3 | async-start | bytes 10485760 | tf_op jit(solution)/shard_map/psum | solution.py:46
  284.5 7.5 copy-start.26
  397.6 207.8 %all-gather.2.cloned.1.call-start = ((), (), s32[]{:S(2)}) async-start(), calls=%async_computation.4 | async-start | bytes 10485760 | tf_op jit(solution)/shard_map/all_gather | solution.py:109
  405.6 120.6 %copy-start.22 = (f32[2560]{0:T(1024)S(1)}, f32[2560]{0:T(1024)}, u32[]{:S(2)}) copy-start(f32[2560]{0:T(1024)} %get-tuple-element.149) | copy-start | bytes 30724
  409.4 133.1 %copy-start.9 = (f32[1024,256]{0,1:T(8,128)}, f32[1024,256]{0,1:T(8,128)S(1)}, u32[]{:S(2)}) copy-start(f32[1024,256]{0,1:T(8,128)S(1)} %get-tuple-element.202) | copy-start | bytes 3145732
  409.4 133.1 %copy-start.11 = (f32[1024,256]{0,1:T(8,128)}, f32[1024,256]{0,1:T(8,128)S(1)}, u32[]{:S(2)}) copy-start(f32[1024,256]{0,1:T(8,128)S(1)} %get-tuple-element.203) | copy-start | bytes 3145732
  531.7 9.7 copy-start
  531.7 9.7 copy-start.28
  571.6 6.7 copy-start.17
  580.7 24.7 %copy-start.13 = (bf16[1024,2,256]{0,2,1:T(8,128)(2,1)}, bf16[1024,2,256]{0,2,1:T(8,128)(2,1)S(1)}, u32[]{:S(2)}) copy-start(bf16[1024,2,256]{0,2,1:T(8,128)(2,1)S(1)} %fusion.165) | copy-start | bytes 3145732
  1174.9 189.7 %all-to-all-start = ((f32[4,1024,2,2,256]{4,1,3,2,0:T(8,128)}), f32[4,1024,2,2,256]{4,1,3,2,0:T(8,128)}, u32[]{:S(2)}, u32[]{:S(2)}) async-start(f32[4,1024,2,2,256]{4,1,3,2,0:T(8,128)} %get-tuple-element.63), calls=%async_computation | async-start | bytes 33554432 | tf_op jit(solution)/shard_map/all_to_all | solution.py:119
  1181.9 328.5 %all-reduce.9.cloned.1.call-start = ((), (), s32[]{:S(2)}) async-start(), calls=%async_computation.5 | async-start | bytes 10485760 | tf_op jit(solution)/shard_map/psum | solution.py:40
  1385.5 128.6 %copy-start.21 = (f32[2560]{0:T(1024)S(1)}, f32[2560]{0:T(1024)}, u32[]{:S(2)}) copy-start(f32[2560]{0:T(1024)} %get-tuple-element.147) | copy-start | bytes 30724
  1385.5 367.3 %all-reduce.11.cloned.1.call-start = ((), (), s32[]{:S(2)}) async-start(), calls=%async_computation.6 | async-start | bytes 10485760 | tf_op jit(solution)/shard_map/psum | solution.py:46
  1514.5 7.6 copy-start.24
  1628.0 7.5 copy-start.18
  1628.0 9.5 copy-start.14
  1631.8 124.8 %copy-start.20 = (f32[2560]{0:T(1024)S(1)}, f32[2560]{0:T(1024)}, u32[]{:S(2)}) copy-start(f32[2560]{0:T(1024)} %get-tuple-element.146) | copy-start | bytes 30724
  (16 other events, 56.6 us)
Sparse Core Ops, SparseCore 0:
  155.6 124.7 all-reduce.4
  397.7 124.6 all-reduce.6
  549.6 55.7 all-gather.1
  1385.7 124.6 all-reduce.8
  1628.1 124.6 all-reduce.10
where the time goes:
time: 1780 us; the launch traced here: 1770 us
  matrix products  718 us (40%)
  waiting for transfers between devices  683 us (38%)
  other arithmetic  247 us (14%)
  local copies, waits for them, and re-layouts  82.7 us (5%)
    psum x2, waiting for transfers between devices, finish(): lax.psum(jnp.dot(attn_out.reshape(row_count, -1), w_out, preferred_elemen...  250 us
    psum x2, waiting for transfers between devices, finish(): lax.psum(jnp.dot(hidden_act, w_down, preferred_element_type=jnp.float32)....  226 us
    all_to_all x1, waiting for transfers between devices, spread_attention(): got_out = lax.all_to_all(part_out, 'cp', 0, 0, tiled=True)  182 us
    reduce_sum x8, other arithmetic, partial_block(): row_sum = cache_exp.sum(axis=-1) + own_exp.sum(axis=-1)  156 us
    dot_general x4, matrix products, partial_block(): jnp.einsum('qkgt,tkd->qkgd', cache_exp.astype(jnp.bfloat16), cache_v, pre...  155 us
    dot_general x4, matrix products, partial_block(): jnp.einsum('qkgd,tkd->qkgt', block_q, cache_k, preferred_element_type=jnp...  152 us
    dot_general x2, matrix products, finish(): up_proj = jnp.dot(normed, w_up, preferred_element_type=jnp.float32)  76.6 us
    dot_general x2, matrix products, finish(): jnp.dot(hidden_act, w_down, preferred_element_type=jnp.float32)  69.4 us
  transfers between devices with their start and end apart: 8, of which 6 were waited for; matrix products, arithmetic and copies ran while one was open for 8% of the time, Pallas kernels for 0%

commit v1 on v0

v1 whole, which is shorter than its diff:
```python
import functools

import jax
import jax.numpy as jnp
from jax import lax
from jax.experimental import pallas as pl
from jax.experimental.pallas import tpu as pltpu
from jax.sharding import PartitionSpec as P

F32 = jnp.float32
BF16 = jnp.bfloat16
EPS = 1e-6
NEG = -1e30
LOG2E = 1.4426950408889634
HD = 256
VMEM_MAX = 63 * 2**20
ROW = ('arbitrary',)


def cost(flops, nbytes, trans=0):
    return pl.CostEstimate(flops=int(flops), bytes_accessed=int(nbytes), transcendentals=int(trans))


def params(n_axes):
    return pltpu.CompilerParams(dimension_semantics=('arbitrary',) * n_axes, vmem_limit_bytes=VMEM_MAX)


def rms(t, gain):
    return t * lax.rsqrt(jnp.mean(t * t, axis=-1, keepdims=True) + EPS) * (1.0 + gain)


def qkv_kernel(combine, n_q, n_kv, *refs):
    if combine:
        (x_ref, d0_ref, d1_ref, gd_ref, g_ref, qk_ref, wq_ref, wk_ref, wv_ref, cos_ref, sin_ref), rest = refs[:11], refs[11:]
    else:
        (x_ref, g_ref, qk_ref, wq_ref, wk_ref, wv_ref, cos_ref, sin_ref), rest = refs[:8], refs[8:]
    n_out = 4 if combine else 3
    outs = rest[len(rest) - n_out:]
    q_ref, k_ref, v_ref = outs[:3]
    x = x_ref[...].astype(F32)
    if combine:
        d = (d0_ref[...].astype(F32) + d1_ref[...].astype(F32)).astype(BF16).astype(F32)
        mid = (x + rms(d, gd_ref[...])).astype(BF16)
        outs[3][...] = mid
        x = mid.astype(F32)
    h = rms(x, g_ref[...]).astype(BF16)
    cos, sin = cos_ref[...], sin_ref[...]

    def turn(t, gain):
        t = rms(t, gain)
        lo, hi = t[:, :HD // 2], t[:, HD // 2:]
        return jnp.concatenate([lo * cos - hi * sin, hi * cos + lo * sin], axis=1).astype(BF16)

    kf = jnp.dot(h, wk_ref[0], preferred_element_type=F32)
    for n in range(n_kv):
        k_ref[:, n * HD:(n + 1) * HD] = turn(kf[:, n * HD:(n + 1) * HD], qk_ref[1:2, :])
    v_ref[...] = jnp.dot(h, wv_ref[0], preferred_element_type=F32).astype(BF16)
    qf = jnp.dot(h, wq_ref[0], preferred_element_type=F32)
    for n in range(n_q):
        q_ref[n] = turn(qf[:, n * HD:(n + 1) * HD], qk_ref[0:1, :])


def qkv(layer, x, d_pair, gd, gain, qk, wq, wk, wv, cos, sin, total_rows, row0, carried, tile=256):
    rows, dim = x.shape
    n_q, n_kv = wq.shape[2] // HD, wk.shape[2] // HD
    combine = d_pair is not None
    t0 = row0 // tile
    rowb = pl.BlockSpec((tile, dim), lambda i: (i, 0))
    vec = pl.BlockSpec((1, dim), lambda i: (0, 0))
    wspec = lambda w: pl.BlockSpec((1, dim, w.shape[2]), lambda i: (layer, 0, 0))
    trig = pl.BlockSpec((tile, HD // 2), lambda i: (i + t0, 0))
    ins, specs = [x], [rowb]
    if combine:
        ins += [d_pair[0], d_pair[1], gd]
        specs += [rowb, rowb, vec]
    ins += [gain, qk, wq, wk, wv, cos, sin]
    specs += [vec, pl.BlockSpec((2, HD), lambda i: (0, 0)), wspec(wq), wspec(wk), wspec(wv), trig, trig]
    aliases = {}
    if carried is not None:
        for j, arr in enumerate(carried):
            aliases[len(ins)] = j
            ins.append(arr)
            specs.append(pl.BlockSpec(memory_space=pl.ANY))
    out_shape = [jax.ShapeDtypeStruct((n_q, total_rows, HD), BF16), jax.ShapeDtypeStruct((total_rows, n_kv * HD), BF16), jax.ShapeDtypeStruct((total_rows, n_kv * HD), BF16)]
    out_specs = [pl.BlockSpec((n_q, tile, HD), lambda i: (0, i + t0, 0)), pl.BlockSpec((tile, n_kv * HD), lambda i: (i + t0, 0)), pl.BlockSpec((tile, n_kv * HD), lambda i: (i + t0, 0))]
    if combine:
        out_shape.append(jax.ShapeDtypeStruct((rows, dim), BF16))
        out_specs.append(rowb)
    cols = (n_q + 2 * n_kv) * HD
    return pl.pallas_call(
        functools.partial(qkv_kernel, combine, n_q, n_kv),
        grid=(rows // tile,), in_specs=specs, out_specs=out_specs, out_shape=out_shape,
        input_output_aliases=aliases, compiler_params=params(1),
        cost_estimate=cost(2 * rows * dim * cols, 2 * (rows * dim + dim * cols + rows * cols)), name='qkv')(*ins)


def window_kernel(tile, tiles, win, q_ref, kp_ref, vp_ref, ko_ref, vo_ref, o_ref):
    scale = LOG2E * HD ** -0.5
    rows2 = 2 * tile
    row = lax.broadcasted_iota(jnp.int32, (rows2, tile), 0) & (tile - 1)
    col = lax.broadcasted_iota(jnp.int32, (rows2, tile), 1)
    nb = win // tile
    for j, t in enumerate(tiles):
        q = q_ref[:, t * tile:(t + 1) * tile, :].reshape(rows2, HD)
        pieces = []
        for b in range(t, t + nb + 1):
            pieces.append((kp_ref, vp_ref, b * tile) if b < nb else (ko_ref, vo_ref, (b - nb) * tile))
        ss = []
        for i, (kr, _, st) in enumerate(pieces):
            s = lax.dot_general(q, kr[st:st + tile, :], (((1,), (1,)), ((), ())), preferred_element_type=F32) * scale
            if i == 0:
                s = jnp.where(col > row, s, NEG)
            if i == nb:
                s = jnp.where(col <= row, s, NEG)
            ss.append(s)
        top = ss[0]
        for s in ss[1:]:
            top = jnp.maximum(top, s)
        top = top.max(axis=1, keepdims=True)
        total = jnp.zeros((rows2, tile), F32)
        acc = jnp.zeros((rows2, HD), F32)
        for s, (_, vr, st) in zip(ss, pieces):
            p = jnp.exp2(s - top)
            total = total + p
            acc = acc + jnp.dot(p.astype(BF16), vr[st:st + tile, :], preferred_element_type=F32)
        out = (acc / total.sum(axis=1, keepdims=True)).astype(BF16)
        for g in range(2):
            o_ref[j * tile:(j + 1) * tile, g * HD:(g + 1) * HD] = out[g * tile:(g + 1) * tile]


def window_attention(q, kp, vp, ko, vo, row0, rows, tile=256):
    n_q = q.shape[0]
    n_kv = n_q // 2
    win = kp.shape[0]
    total = q.shape[1]
    tiles = tuple(range(row0 // tile, (row0 + rows) // tile))
    kv = lambda n: pl.BlockSpec((n, HD), lambda h: (0, h))
    return pl.pallas_call(
        functools.partial(window_kernel, tile, tiles, win),
        grid=(n_kv,),
        in_specs=[pl.BlockSpec((2, total, HD), lambda h: (h, 0, 0)), kv(win), kv(win), kv(total), kv(total)],
        out_specs=pl.BlockSpec((rows, 2 * HD), lambda h: (0, h)),
        out_shape=jax.ShapeDtypeStruct((rows, n_q * HD), BF16),
        compiler_params=params(1),
        cost_estimate=cost(4 * rows * n_q * (win + tile) * HD, 2 * (4 * total * n_kv * HD + 2 * rows * n_q * HD)), name='window')(q, kp, vp, ko, vo)


def split3(x):
    hi = x.astype(BF16)
    r = x - hi.astype(F32)
    mid = r.astype(BF16)
    return hi, mid, (r - mid.astype(F32)).astype(BF16)


def global_kernel(bq, bk, ns, sc_ref, q_ref, kc_ref, vc_ref, kn_ref, vn_ref, o_ref, aux_ref, m_ref, l_ref, acc_ref):
    head = pl.program_id(0)
    qt = pl.program_id(1)
    n_valid = sc_ref[0]
    delta = sc_ref[1]
    scale = LOG2E * HD ** -0.5
    m_ref[...] = jnp.full_like(m_ref, NEG)
    l_ref[...] = jnp.zeros_like(l_ref)
    acc_ref[...] = jnp.zeros_like(acc_ref)
    rs = 2 * bq // ns

    def block(k_ref, v_ref, start, mask_fn):
        k = k_ref[pl.ds(start, bk), :]
        v = v_ref[pl.ds(start, bk), :]
        ss = []
        for c in range(ns):
            g, r0 = divmod(c * rs, bq)
            s = lax.dot_general(q_ref[g, r0:r0 + rs, :], k, (((1,), (1,)), ((), ())), preferred_element_type=F32) * scale
            if mask_fn is not None:
                s = jnp.where(mask_fn(r0, rs), s, NEG)
            ss.append(s)
        for c, s in enumerate(ss):
            rows = slice(c * rs, (c + 1) * rs)
            m_prev = m_ref[rows, :]
            m_new = jnp.maximum(m_prev, s.max(axis=1, keepdims=True))
            alpha = jnp.exp2(m_prev - m_new)
            l = l_ref[rows, :] * alpha
            ps = []
            for j in range(bk // 128):
                p = jnp.exp2(s[:, j * 128:(j + 1) * 128] - m_new)
                l = l + p
                ps.append(p.astype(BF16))
            l_ref[rows, :] = l
            m_ref[rows, :] = m_new
            pv = jnp.dot(jnp.concatenate(ps, axis=1), v, preferred_element_type=F32)
            for j in range(HD // 128):
                cs = slice(j * 128, (j + 1) * 128)
                acc_ref[rows, cs] = acc_ref[rows, cs] * alpha + pv[:, cs]

    n_full = n_valid // bk

    def cache_step(i, c):
        block(kc_ref, vc_ref, pl.multiple_of(i * bk, bk), None)
        return c

    lax.fori_loop(0, n_full, cache_step, 0)

    @pl.when(n_full * bk < n_valid)
    def _():
        start = pl.multiple_of(n_full * bk, bk)
        block(kc_ref, vc_ref, start, lambda r0, n: (start + lax.broadcasted_iota(jnp.int32, (n, bk), 1)) < n_valid)

    n_new = kn_ref.shape[0]
    row0 = qt * bq + delta
    own_full = jnp.clip((row0 + 1) // bk, 0, n_new // bk)
    own_any = jnp.clip((row0 + bq + bk - 1) // bk, 0, n_new // bk)

    def own_step(i, c):
        block(kn_ref, vn_ref, pl.multiple_of(i * bk, bk), None)
        return c

    lax.fori_loop(0, own_full, own_step, 0)

    def diag_step(i, c):
        start = pl.multiple_of(i * bk, bk)

        def mask(r0, n):
            key = start + lax.broadcasted_iota(jnp.int32, (n, bk), 1)
            return key <= row0 + r0 + lax.broadcasted_iota(jnp.int32, (n, bk), 0)

        block(kn_ref, vn_ref, start, mask)
        return c

    lax.fori_loop(own_full, own_any, diag_step, 0)
    lane = lax.broadcasted_iota(jnp.int32, (bq, 128), 1)
    row_sl = pl.ds(pl.multiple_of(qt * bq, bq), bq)
    aux = aux_ref[row_sl, :]
    for g in range(2):
        rows = slice(g * bq, (g + 1) * bq)
        l = l_ref[rows, :].sum(axis=1, keepdims=True)
        o_ref[:, g * HD:(g + 1) * HD] = (acc_ref[rows, :] / l).astype(BF16)
        lse = m_ref[rows, :] + jnp.log2(l)
        for p, part in enumerate(split3(lse)):
            aux = jnp.where(lane == 16 * (2 * head + g) + p, part, aux)
    aux_ref[row_sl, :] = aux


def global_attention(q, kc, vc, kn, vn, sc, bk=1024, ns=4):
    n_q, rows, _ = q.shape
    bq = min(rows, 1024)
    n_kv = n_q // 2
    kv = lambda a: pl.BlockSpec((a.shape[0], HD), lambda h, t, *_: (0, h))
    keys = kc.shape[0] + kn.shape[0]
    return pl.pallas_call(
        functools.partial(global_kernel, bq, bk, ns),
        grid_spec=pltpu.PrefetchScalarGridSpec(
            num_scalar_prefetch=1, grid=(n_kv, rows // bq),
            in_specs=[pl.BlockSpec((2, bq, HD), lambda h, t, *_: (h, t, 0)), kv(kc), kv(vc), kv(kn), kv(vn)],
            out_specs=[pl.BlockSpec((bq, 2 * HD), lambda h, t, *_: (t, h)), pl.BlockSpec((rows, 128), lambda h, t, *_: (0, 0))],
            scratch_shapes=[pltpu.VMEM((2 * bq, 128), F32), pltpu.VMEM((2 * bq, 128), F32), pltpu.VMEM((2 * bq, HD), F32)]),
        out_shape=[jax.ShapeDtypeStruct((rows, n_q * HD), BF16), jax.ShapeDtypeStruct((rows, 128), BF16)],
        compiler_params=params(2),
        cost_estimate=cost(4 * rows * n_q * keys * HD, 2 * (2 * keys * n_kv * HD + 2 * rows * n_q * HD), rows * n_q * keys),
        name='gattn')(sc, q, kc, vc, kn, vn)


def merge_kernel(n, n_q, *refs):
    parts, auxs = refs[:n], refs[n:2 * n]
    o_ref = refs[2 * n]
    aux_out = refs[2 * n + 1] if len(refs) > 2 * n + 1 else None
    rows = o_ref.shape[0]
    lane = lax.broadcasted_iota(jnp.int32, (rows, 128), 1)
    new_aux = jnp.zeros((rows, 128), BF16)
    for h in range(n_q):
        lses = []
        for a in auxs:
            c = a[:, 16 * h:16 * h + 3].astype(F32)
            lses.append(c[:, 0:1] + c[:, 1:2] + c[:, 2:3])
        top = functools.reduce(jnp.maximum, lses)
        ws = [jnp.exp2(s - top) for s in lses]
        total = functools.reduce(jnp.add, ws)
        cs = slice(h * HD, (h + 1) * HD)
        o = functools.reduce(jnp.add, [p[:, cs].astype(F32) * (w / total) for p, w in zip(parts, ws)])
        o_ref[:, cs] = o.astype(BF16)
        if aux_out is not None:
            lse = jnp.broadcast_to(top + jnp.log2(total), (rows, 128))
            for p, part in enumerate(split3(lse)):
                new_aux = jnp.where(lane == 16 * h + p, part, new_aux)
    if aux_out is not None:
        aux_out[...] = new_aux


def merge(parts, row0, rows, keep_aux, tile=256):
    n = len(parts)
    width = parts[0][0].shape[1]
    t0 = row0 // tile
    big = lambda i: (i + t0, 0)
    out_shape = [jax.ShapeDtypeStruct((rows, width), BF16)]
    out_specs = [pl.BlockSpec((tile, width), lambda i: (i, 0))]
    if keep_aux:
        out_shape.append(jax.ShapeDtypeStruct((rows, 128), BF16))
        out_specs.append(pl.BlockSpec((tile, 128), lambda i: (i, 0)))
    return pl.pallas_call(
        functools.partial(merge_kernel, n, width // HD), grid=(rows // tile,),
        in_specs=[pl.BlockSpec((tile, width), big)] * n + [pl.BlockSpec((tile, 128), big)] * n,
        out_specs=out_specs, out_shape=out_shape, compiler_params=params(1),
        cost_estimate=cost(8e6, 2 * (n + 1) * rows * width), name='merge')(*[p[0] for p in parts], *[p[1] for p in parts])


def wo_kernel(tp_ref, x_ref, o0_ref, o1_ref, w_ref, ga_ref, gu_ref, x1_ref, u_ref):
    own, other = o0_ref[...], o1_ref[...]
    first = tp_ref[0] == 0
    o = jnp.concatenate([jnp.where(first, own, other), jnp.where(first, other, own)], axis=1)
    a = jnp.dot(o, w_ref[...], preferred_element_type=F32).astype(BF16).astype(F32)
    x1 = (x_ref[...].astype(F32) + rms(a, ga_ref[...])).astype(BF16)
    x1_ref[...] = x1
    u_ref[...] = rms(x1.astype(F32), gu_ref[...]).astype(BF16)


def out_proj(tp, x, o_own, o_other, w, ga, gu, row0, tile=256):
    rows, half = o_own.shape
    dim = w.shape[1]
    t0 = row0 // tile
    rowb = pl.BlockSpec((tile, dim), lambda i, *_: (i, 0))
    vec = pl.BlockSpec((1, dim), lambda i, *_: (0, 0))
    ob = pl.BlockSpec((tile, half), lambda i, *_: (i, 0))
    return pl.pallas_call(
        wo_kernel,
        grid_spec=pltpu.PrefetchScalarGridSpec(
            num_scalar_prefetch=1, grid=(rows // tile,),
            in_specs=[pl.BlockSpec((tile, dim), lambda i, *_: (i + t0, 0)), ob, ob, pl.BlockSpec(w.shape, lambda i, *_: (0, 0)), vec, vec],
            out_specs=[rowb, rowb]),
        out_shape=[jax.ShapeDtypeStruct((rows, dim), BF16)] * 2, compiler_params=params(1),
        cost_estimate=cost(4 * rows * half * dim, 2 * (2 * half * dim + 3 * rows * dim)), name='wo')(tp, x, o_own, o_other, w, ga, gu)


def ffn_kernel(nb, u_ref, wg_ref, wu_ref, wd_ref, d_ref, act_ref, acc_ref):
    n = pl.program_id(0)

    def head(slot):
        g = jnp.dot(u_ref[...], wg_ref[0], preferred_element_type=F32)
        up = jnp.dot(u_ref[...], wu_ref[0], preferred_element_type=F32)
        act_ref[slot] = (jax.nn.gelu(g, approximate=True) * up).astype(BF16)

    def tail(slot):
        return jnp.dot(act_ref[slot], wd_ref[0], preferred_element_type=F32)

    @pl.when(n == 0)
    def _():
        head(0)
        acc_ref[...] = jnp.zeros_like(acc_ref)

    for slot in range(2):
        @pl.when((n > 0) & (n < nb) & (n % 2 == slot))
        def _():
            acc_ref[...] += tail(1 - slot)
            head(slot)

    @pl.when(n == nb)
    def _():
        d_ref[...] = (acc_ref[...] + tail((nb - 1) % 2)).astype(BF16)


def ffn(layer, u, wg, wu, wd, bn=512):
    rows, dim = u.shape
    width = wg.shape[2]
    nb = width // bn
    return pl.pallas_call(
        functools.partial(ffn_kernel, nb), grid=(nb + 1,),
        in_specs=[pl.BlockSpec((rows, dim), lambda n: (0, 0)),
                  pl.BlockSpec((1, dim, bn), lambda n: (layer, 0, jnp.minimum(n, nb - 1))),
                  pl.BlockSpec((1, dim, bn), lambda n: (layer, 0, jnp.minimum(n, nb - 1))),
                  pl.BlockSpec((1, bn, dim), lambda n: (layer, jnp.maximum(n - 1, 0), 0))],
        out_specs=pl.BlockSpec((rows, dim), lambda n: (0, 0)),
        out_shape=jax.ShapeDtypeStruct((rows, dim), BF16),
        scratch_shapes=[pltpu.VMEM((2, rows, bn), BF16), pltpu.VMEM((rows, dim), F32)],
        compiler_params=params(1),
        cost_estimate=cost(6 * rows * dim * width, 2 * (3 * dim * width + 2 * rows * dim), rows * width), name='ffn')(u, wg, wu, wd)


def last_kernel(x_ref, d0_ref, d1_ref, g_ref, *rest):
    d = (d0_ref[...].astype(F32) + d1_ref[...].astype(F32)).astype(BF16).astype(F32)
    rest[-1][...] = (x_ref[...].astype(F32) + rms(d, g_ref[...])).astype(BF16)


def last(x, d_pair, gain, total_rows, row0, carried, tile=256):
    rows, dim = x.shape
    t0 = row0 // tile
    rowb = pl.BlockSpec((tile, dim), lambda i: (i, 0))
    ins = [x, d_pair[0], d_pair[1], gain]
    specs = [rowb, rowb, rowb, pl.BlockSpec((1, dim), lambda i: (0, 0))]
    aliases = {}
    if carried is not None:
        aliases[4] = 0
        ins.append(carried)
        specs.append(pl.BlockSpec(memory_space=pl.ANY))
    return pl.pallas_call(
        last_kernel, grid=(rows // tile,), in_specs=specs,
        out_specs=pl.BlockSpec((tile, dim), lambda i: (i + t0, 0)),
        out_shape=jax.ShapeDtypeStruct((total_rows, dim), BF16), input_output_aliases=aliases,
        compiler_params=params(1), cost_estimate=cost(10 * rows * dim, 8 * rows * dim), name='last')(*ins)


def rope_tables(positions, base, divisor):
    inv_freq = 1.0 / (base ** (jnp.arange(0, HD, 2, dtype=F32) / HD))
    angles = (positions.astype(F32) / divisor)[:, None] * inv_freq[None, :]
    return jnp.cos(angles), jnp.sin(angles)


def solution(mesh):
    cp_size = mesh.shape['cp']
    tp_size = mesh.shape['tp']
    row_spec = P(('dp', 'cp'), None)
    cache_spec = P(('dp', 'cp'), 'tp', None)
    window_spec = P('dp', 'tp', None)
    col_spec = P(None, None, 'tp')
    row_split = P(None, 'tp', None)
    replicated = P()
    swap_tp = [(i, tp_size - 1 - i) for i in range(tp_size)]
    chunks = 2

    def xor(k):
        return [(i, i ^ k) for i in range(cp_size)]

    def device_step(hidden, start_pos, k_local, v_local, k_global, v_global, w_query, w_key, w_value, w_out, w_gate, w_up, w_down, norm_gain, qk_gain):
        first_pos = start_pos[0]
        cp_index = lax.axis_index('cp')
        tp_index = lax.axis_index('tp')
        tp = tp_index.astype(jnp.int32)[None]
        rows = hidden.shape[0]
        part = rows // chunks
        n_kv = k_local.shape[1]
        shard_len = k_global.shape[0]
        positions = first_pos + cp_index * rows + jnp.arange(rows)
        gains = lambda l, i: norm_gain[l, i][None, :]

        quarter = w_out.shape[1] // cp_size
        w_full = []
        for l in range(2):
            piece = lax.dynamic_slice(w_out, (l, cp_index * quarter, 0), (1, quarter, w_out.shape[2]))[0]
            w_full.append(lax.all_gather(piece, ('tp', 'cp'), axis=0, tiled=True))

        def finish(l, x_of, o_parts):
            xs, us, ds = [], [], []
            others = [lax.ppermute(o, 'tp', swap_tp) for o in o_parts]
            for i in range(chunks):
                x, r0 = x_of(i)
                x1, u = out_proj(tp, x, o_parts[i], others[i], w_full[l], gains(l, 1), gains(l, 2), r0)
                d = ffn(l, u, w_gate, w_up, w_down)
                xs.append(x1)
                ds.append((d, lax.ppermute(d, 'tp', swap_tp)))
            return xs, ds

        cos, sin = rope_tables(positions, 10000.0, 1.0)
        q, k_loc, v_loc = qkv(0, hidden, None, None, gains(0, 0), qk_gain[0], w_query, w_key, w_value, cos, sin, rows, 0, None)
        ahead = [(i, i + 1) for i in range(cp_size - 1)]
        shift = jnp.remainder(first_pos, k_local.shape[0])

        def before(cache, new):
            rolled = jnp.roll(cache.reshape(cache.shape[0], -1), -shift, axis=0)
            return jnp.where(cp_index == 0, rolled, lax.ppermute(new, 'cp', ahead))

        k_prev, v_prev = before(k_local, k_loc), before(v_local, v_loc)
        o_parts = [window_attention(q, k_prev, v_prev, k_loc, v_loc, i * part, part) for i in range(chunks)]
        xs, ds = finish(0, lambda i: (hidden, i * part), o_parts)

        cos, sin = rope_tables(positions, 1000000.0, 8.0)
        carried, mids = None, []
        for i in range(chunks):
            *carried, mid = qkv(1, xs[i], ds[i], gains(0, 3), gains(1, 0), qk_gain[1], w_query, w_key, w_value, cos, sin, rows, i * part, carried)
            mids.append(mid)
        q, k_glob, v_glob = carried
        kc = k_global.reshape(shard_len, -1)
        vc = v_global.reshape(shard_len, -1)
        n_valid = jnp.clip(first_pos - cp_index * shard_len, 0, shard_len)

        def attend(block_q, owner):
            sc = jnp.stack([n_valid, (owner - cp_index) * rows]).astype(jnp.int32)
            return global_attention(block_q, kc, vc, k_glob, v_glob, sc)

        def move(pair, k):
            return [lax.ppermute(a, 'cp', xor(k)) for a in pair]

        q2 = lax.ppermute(q, 'cp', xor(2))
        q1 = lax.ppermute(q, 'cp', xor(1))
        q3 = lax.ppermute(q2, 'cp', xor(1))
        own = attend(q, cp_index)
        far3 = attend(q3, cp_index ^ 3)
        far2 = attend(q2, cp_index ^ 2)
        near = attend(q1, cp_index ^ 1)
        far = move(merge([far2, move(far3, 1)], 0, rows, True), 2)
        near = move(near, 1)
        o_parts = [merge([own, near, far], i * part, part, False)[0] for i in range(chunks)]
        xs, ds = finish(1, lambda i: (mids[i], 0), o_parts)
        out = None
        for i in range(chunks):
            out = last(xs[i], ds[i], gains(1, 3), rows, i * part, out)
        heads = lambda a: a.reshape(rows, n_kv, HD)
        return out, heads(k_loc), heads(v_loc), heads(k_glob), heads(v_glob)

    return jax.shard_map(device_step, mesh=mesh, in_specs=(row_spec, P('dp'), window_spec, window_spec, cache_spec, cache_spec, col_spec, col_spec, col_spec, row_split, col_spec, col_spec, row_split, replicated, replicated), out_specs=(row_spec, cache_spec, cache_spec, cache_spec, cache_spec), check_vma=False)
```

time: 1780 us -> 796 us (0.45)
  matrix products: 718 us -> 0 us
  waiting for transfers between devices: 683 us -> 121 us
  Pallas kernels: 0 us -> 554 us
  other arithmetic: 247 us -> 14.7 us
  local copies, waits for them, and re-layouts: 82.7 us -> 26.2 us
  starting transfers between devices: 15.9 us -> 57.8 us
    dot_general x31 -> x0, matrix products: 690 us -> none  [the longest x4 155 us: partial_block(): jnp.einsum('qkgt,tkd->qkgd', cache_exp.astype(jnp.bfloat16), cache_v, pre...]
    pallas_call x0 -> x22, Pallas kernels: none -> 554 us  [the longest x4 202 us: global_attention(): pl.pallas_call(functools.partial(global_kernel, bq, bk, ns), grid_spec=pl...]
    psum x4 -> x0, waiting for transfers between devices: 476 us -> none  [the longest x2 250 us: finish(): lax.psum(jnp.dot(attn_out.reshape(row_count, -1), w_out, preferred_elemen...]
    reduce_sum x18 -> x0, other arithmetic: 198 us -> none  [the longest x8 156 us: partial_block(): row_sum = cache_exp.sum(axis=-1) + own_exp.sum(axis=-1)]
    all_to_all x1 -> x0, waiting for transfers between devices: 182 us -> none  [spread_attention(): got_out = lax.all_to_all(part_out, 'cp', 0, 0, tiled=True)]
    ppermute x2 -> x19, waiting for transfers between devices: 0.01 us -> 121 us  [the longest x4 67.2 us: finish(): ds.append((d, lax.ppermute(d, 'tp', swap_tp)))]
    ppermute x2 -> x19, starting transfers between devices: 8.53 us -> 57.7 us  [the longest x1 38.2 us: device_step(): q2 = lax.ppermute(q, 'cp', xor(2))]
    dot_general x6 -> x0, local copies, waits for them, and re-layouts: 33 us -> none  [the longest x3 25.1 us: project(): jnp.dot(normed, w_query, preferred_element_type=jnp.float32)]
  transfers between devices with their start and end apart: 8 -> 21, of which waited for: 6 -> 5; matrix products, arithmetic and copies ran while one was open for 8% -> 5% of each run, Pallas kernels for 0% -> 70%
where the time goes in v1:
time: 796 us; the launch traced here: 789 us
  Pallas kernels  554 us (70%)
  waiting for transfers between devices  121 us (15%)
  starting transfers between devices  57.8 us (7%)
  local copies, waits for them, and re-layouts  26.2 us (3%)
  between operations  15.3 us (2%)
  other arithmetic  14.7 us (2%)
    pallas_call x4, Pallas kernels, global_attention(): pl.pallas_call(functools.partial(global_kernel, bq, bk, ns), grid_spec=pl...  202 us
    pallas_call x4, Pallas kernels, ffn(): pl.pallas_call(functools.partial(ffn_kernel, nb), grid=(nb + 1,), in_spec...  201 us
    ppermute x4, waiting for transfers between devices, finish(): ds.append((d, lax.ppermute(d, 'tp', swap_tp)))  67.2 us
    pallas_call x4, Pallas kernels, out_proj(): pl.pallas_call(wo_kernel, grid_spec=pltpu.PrefetchScalarGridSpec(num_scal...  55.5 us
    pallas_call x3, Pallas kernels, qkv(): pl.pallas_call(functools.partial(qkv_kernel, combine, n_q, n_kv), grid=(r...  50.7 us
    ppermute x1, starting transfers between devices, device_step(): q2 = lax.ppermute(q, 'cp', xor(2))  38.2 us
    ppermute x4, waiting for transfers between devices, finish(): others = [lax.ppermute(o, 'tp', swap_tp) for o in o_parts]  29.2 us
    ppermute x1, waiting for transfers between devices, device_step(): q2 = lax.ppermute(q, 'cp', xor(2))  24.4 us
  transfers between devices with their start and end apart: 21, of which 5 were waited for; matrix products, arithmetic and copies ran while one was open for 5% of the time, Pallas kernels for 70%

profile of v1, /device:TPU:0, one launch (start us, length us, event | category | flops | bytes accessed | tf_op | source)
XLA Modules:
  0.0 788.9 jit_solution(4153571490013727279)
XLA Ops:
  15.7 19.2 %qkv.3 = (bf16[4,1024,256]{2,1,0:T(8,128)(2,1)}, bf16[1024,512]{1,0:T(8,128)(2,1)}, bf16[1024,512]{1,0:T(8,128)(2,1)}) custom-call(bf16[1024,2560]{1,0:T(8,128)(2,1)} %x_ref.3, f32[1,2560]{1,0:T(1,128)} %get-tuple-element.72.refs_1_, f32[2,256]{1,0:T(2,128)} %get-tuple-element.79.refs_2_, bf16[2,2560,1024]{2,1,0:T(8,128)(2,1)} %refs_6_.3, ...), custom_call_target="tpu_custom_call" | custom-call | flops 10737418240 | bytes 19922944 | tf_op jit(solution)/shard_map/qkv/pallas_call | solution.py:90
  51.3 8.6 %window.3.o0_ref = bf16[512,1024]{1,0:T(8,128)(2,1)} custom-call(bf16[4,1024,256]{2,1,0:T(8,128)(2,1)} %get-tuple-element.35.q_ref, bf16[1024,512]{1,0:T(8,128)(2,1)} %fusion.3.kp_ref, bf16[1024,512]{1,0:T(8,128)(2,1)} %fusion.1.vp_ref, bf16[1024,512]{1,0:T(8,128)(2,1)} %get-tuple-element.36.ko_ref, bf16[1024,512]{1,0:T(8,128)(2,1)} %get-tuple-element.37.vo_ref), custom_call_target="tpu_custom_call" | custom-call | flops 2684354560 | bytes 6291456 | tf_op jit(solution)/shard_map/window/pallas_call | solution.py:138
  61.4 8.2 %window.2.o0_ref = bf16[512,1024]{1,0:T(8,128)(2,1)} custom-call(bf16[4,1024,256]{2,1,0:T(8,128)(2,1)} %get-tuple-element.35.q_ref, bf16[1024,512]{1,0:T(8,128)(2,1)} %fusion.3.kp_ref, bf16[1024,512]{1,0:T(8,128)(2,1)} %fusion.1.vp_ref, bf16[1024,512]{1,0:T(8,128)(2,1)} %get-tuple-element.36.ko_ref, bf16[1024,512]{1,0:T(8,128)(2,1)} %get-tuple-element.37.vo_ref), custom_call_target="tpu_custom_call" | custom-call | flops 2684354560 | bytes 6291456 | tf_op jit(solution)/shard_map/window/pallas_call | solution.py:138
  70.1 10.2 %collective-permute-done.4.o1_ref = bf16[512,1024]{1,0:T(8,128)(2,1)} collective-permute-done((bf16[512,1024]{1,0:T(8,128)(2,1)}, bf16[512,1024]{1,0:T(8,128)(2,1)}, u32[]{:S(2)}, u32[]{:S(2)}) %collective-permute-start.4) | collective-permute-done | bytes 1048608 | tf_op jit(solution)/shard_map/ppermute | solution.py:439
  80.3 13.9 %wo.5 = (bf16[512,2560]{1,0:T(8,128)(2,1)}, bf16[512,2560]{1,0:T(8,128)(2,1)}) custom-call(s32[1]{0:T(128)} %bitcast.tp_ref, bf16[1024,2560]{1,0:T(8,128)(2,1)} %x_ref.3, bf16[512,1024]{1,0:T(8,128)(2,1)} %window.3.o0_ref, bf16[512,1024]{1,0:T(8,128)(2,1)} %collective-permute-done.4.o1_ref, bf16[2048,2560]{1,0:T(8,128)(2,1)} %bitcast.57, ...), custom_call_target="tpu_custom_call" | custom-call | flops 5368709120 | bytes 18350080 | tf_op jit(solution)/shard_map/wo/pallas_call | solution.py:321
  94.2 50.2 %ffn.5.refs_1_ = bf16[512,2560]{1,0:T(8,128)(2,1)} custom-call(bf16[512,2560]{1,0:T(8,128)(2,1)} %get-tuple-element.41.u_ref, bf16[2,2560,5120]{2,1,0:T(8,128)(2,1)} %wg_ref.7, bf16[2,2560,5120]{2,1,0:T(8,128)(2,1)} %wu_ref.7, bf16[2,5120,2560]{2,1,0:T(8,128)(2,1)} %wd_ref.7), custom_call_target="tpu_custom_call" | custom-call | flops 40265318400 | bytes 83886080 | tf_op jit(solution)/shard_map/ffn/pallas_call | solution.py:362
  146.1 13.9 %wo.4 = (bf16[512,2560]{1,0:T(8,128)(2,1)}, bf16[512,2560]{1,0:T(8,128)(2,1)}) custom-call(s32[1]{0:T(128)} %bitcast.tp_ref, bf16[1024,2560]{1,0:T(8,128)(2,1)} %x_ref.3, bf16[512,1024]{1,0:T(8,128)(2,1)} %window.2.o0_ref, bf16[512,1024]{1,0:T(8,128)(2,1)} %collective-permute-done.2.o1_ref, bf16[2048,2560]{1,0:T(8,128)(2,1)} %bitcast.58, ...), custom_call_target="tpu_custom_call" | custom-call | flops 5368709120 | bytes 18350080 | tf_op jit(solution)/shard_map/wo/pallas_call | solution.py:321
  160.0 50.4 %ffn.4.refs_1_ = bf16[512,2560]{1,0:T(8,128)(2,1)} custom-call(bf16[512,2560]{1,0:T(8,128)(2,1)} %get-tuple-element.39.u_ref, bf16[2,2560,5120]{2,1,0:T(8,128)(2,1)} %wg_ref.7, bf16[2,2560,5120]{2,1,0:T(8,128)(2,1)} %wu_ref.7, bf16[2,5120,2560]{2,1,0:T(8,128)(2,1)} %wd_ref.7), custom_call_target="tpu_custom_call" | custom-call | flops 40265318400 | bytes 83886080 | tf_op jit(solution)/shard_map/ffn/pallas_call | solution.py:362
  213.7 15.9 %qkv.4 = (bf16[4,1024,256]{2,1,0:T(8,128)(2,1)}, bf16[1024,512]{1,0:T(8,128)(2,1)}, bf16[1024,512]{1,0:T(8,128)(2,1)}, bf16[512,2560]{1,0:T(8,128)(2,1)}) custom-call(bf16[512,2560]{1,0:T(8,128)(2,1)} %get-tuple-element.40.refs_0_, bf16[512,2560]{1,0:T(8,128)(2,1)} %ffn.5.refs_1_, bf16[512,2560]{1,0:T(8,128)(2,1)} %collective-permute-done.5.refs_2_, ...), custom_call_target="tpu_custom_call" | custom-call | flops 5368709120 | bytes 15204352 | tf_op jit(solution)/shard_map/qkv/pallas_call | solution.py:90
  229.7 24.2 %collective-permute-done.3.refs_2_ = bf16[512,2560]{1,0:T(8,128)(2,1)} collective-permute-done((bf16[512,2560]{1,0:T(8,128)(2,1)}, bf16[512,2560]{1,0:T(8,128)(2,1)}, u32[]{:S(2)}, u32[]{:S(2)}) %collective-permute-start.3) | collective-permute-done | bytes 2621472 | tf_op jit(solution)/shard_map/ppermute | solution.py:445
  253.9 15.6 %qkv.5 = (bf16[4,1024,256]{2,1,0:T(8,128)(2,1)}, bf16[1024,512]{1,0:T(8,128)(2,1)}, bf16[1024,512]{1,0:T(8,128)(2,1)}, bf16[512,2560]{1,0:T(8,128)(2,1)}) custom-call(bf16[512,2560]{1,0:T(8,128)(2,1)} %get-tuple-element.38.refs_0_, bf16[512,2560]{1,0:T(8,128)(2,1)} %ffn.4.refs_1_, ...), custom_call_target="tpu_custom_call", output_to_operand_aliasing={{0}: (11, {}), {1}: (12, {}), {2}: (13, {})} | custom-call | flops 5368709120 | bytes 15204352 | tf_op jit(solution)/shard_map/qkv/pallas_call | solution.py:90
  269.4 38.2 %collective-permute-start.8 = (bf16[4,1024,256]{2,1,0:T(8,128)(2,1)}, bf16[4,1024,256]{2,1,0:T(8,128)(2,1)}, u32[]{:S(2)}, u32[]{:S(2)}) collective-permute-start(bf16[4,1024,256]{2,1,0:T(8,128)(2,1)} %get-tuple-element.46.q_ref), channel_id=1, source_target_pairs={{0,2},{1,3},{2,0},{3,1},{4,6},{5,7},{6,4},{7,5}} | collective-permute-start | bytes 6291464 | tf_op jit(solution)/shard_map/ppermute | solution.py:478
  323.0 24.4 %collective-permute-done.8.q_ref = bf16[4,1024,256]{2,1,0:T(8,128)(2,1)} collective-permute-done((bf16[4,1024,256]{2,1,0:T(8,128)(2,1)}, bf16[4,1024,256]{2,1,0:T(8,128)(2,1)}, u32[]{:S(2)}, u32[]{:S(2)}) %collective-permute-start.8) | collective-permute-done | bytes 2097184 | tf_op jit(solution)/shard_map/ppermute | solution.py:478
  347.4 50.2 %gattn.5 = (bf16[1024,1024]{1,0:T(8,128)(2,1)}, bf16[1024,128]{1,0:T(8,128)(2,1)}) custom-call(s32[2]{0:T(128)} %pad_add_fusion.1.sc_ref, bf16[4,1024,256]{2,1,0:T(8,128)(2,1)} %collective-permute-done.6.q_ref, bf16[6144,512]{1,0:T(8,128)(2,1)} %bitcast.43, bf16[6144,512]{1,0:T(8,128)(2,1)} %bitcast.47, bf16[1024,512]{1,0:T(8,128)(2,1)} %get-tuple-element.47.kn_ref, ...), custom_call_target="tpu_custom_call" | custom-call | flops 30064771072 | bytes 18874368 | tf_op jit(solution)/shard_map/gattn/pallas_call | solution.py:248
  398.1 50.5 %gattn.7 = (bf16[1024,1024]{1,0:T(8,128)(2,1)}, bf16[1024,128]{1,0:T(8,128)(2,1)}) custom-call(s32[2]{0:T(128)} %pad_add_fusion.3.sc_ref, bf16[4,1024,256]{2,1,0:T(8,128)(2,1)} %collective-permute-done.9.q_ref, bf16[6144,512]{1,0:T(8,128)(2,1)} %bitcast.44, bf16[6144,512]{1,0:T(8,128)(2,1)} %bitcast.48, bf16[1024,512]{1,0:T(8,128)(2,1)} %get-tuple-element.47.kn_ref, ...), custom_call_target="tpu_custom_call" | custom-call | flops 30064771072 | bytes 18874368 | tf_op jit(solution)/shard_map/gattn/pallas_call | solution.py:248
  449.2 50.2 %gattn.6 = (bf16[1024,1024]{1,0:T(8,128)(2,1)}, bf16[1024,128]{1,0:T(8,128)(2,1)}) custom-call(s32[2]{0:T(128)} %pad_add_fusion.2.sc_ref, bf16[4,1024,256]{2,1,0:T(8,128)(2,1)} %collective-permute-done.8.q_ref, bf16[6144,512]{1,0:T(8,128)(2,1)} %bitcast.45, bf16[6144,512]{1,0:T(8,128)(2,1)} %bitcast.49, bf16[1024,512]{1,0:T(8,128)(2,1)} %get-tuple-element.47.kn_ref, ...), custom_call_target="tpu_custom_call" | custom-call | flops 30064771072 | bytes 18874368 | tf_op jit(solution)/shard_map/gattn/pallas_call | solution.py:248
  500.1 7.0 merge.3
  509.2 51.2 %gattn.4 = (bf16[1024,1024]{1,0:T(8,128)(2,1)}, bf16[1024,128]{1,0:T(8,128)(2,1)}) custom-call(s32[2]{0:T(128)} %pad_add_fusion.sc_ref, bf16[4,1024,256]{2,1,0:T(8,128)(2,1)} %get-tuple-element.46.q_ref, bf16[6144,512]{1,0:T(8,128)(2,1)} %bitcast.46, bf16[6144,512]{1,0:T(8,128)(2,1)} %bitcast.50, bf16[1024,512]{1,0:T(8,128)(2,1)} %get-tuple-element.47.kn_ref, ...), custom_call_target="tpu_custom_call" | custom-call | flops 30064771072 | bytes 18874368 | tf_op jit(solution)/shard_map/gattn/pallas_call | solution.py:248
  573.3 19.0 %collective-permute-done.17.o1_ref = bf16[512,1024]{1,0:T(8,128)(2,1)} collective-permute-done((bf16[512,1024]{1,0:T(8,128)(2,1)}, bf16[512,1024]{1,0:T(8,128)(2,1)}, u32[]{:S(2)}, u32[]{:S(2)}) %collective-permute-start.17) | collective-permute-done | bytes 1048608 | tf_op jit(solution)/shard_map/ppermute | solution.py:439
  592.2 13.9 %wo.7 = (bf16[512,2560]{1,0:T(8,128)(2,1)}, bf16[512,2560]{1,0:T(8,128)(2,1)}) custom-call(s32[1]{0:T(128)} %bitcast.tp_ref, bf16[512,2560]{1,0:T(8,128)(2,1)} %get-tuple-element.61.x_ref, bf16[512,1024]{1,0:T(8,128)(2,1)} %merge.5.o0_ref, bf16[512,1024]{1,0:T(8,128)(2,1)} %collective-permute-done.17.o1_ref, bf16[2048,2560]{1,0:T(8,128)(2,1)} %bitcast.55, ...), custom_call_target="tpu_custom_call" | custom-call | flops 5368709120 | bytes 18350080 | tf_op jit(solution)/shard_map/wo/pallas_call | solution.py:321
  606.1 49.9 %ffn.7.d0_ref = bf16[512,2560]{1,0:T(8,128)(2,1)} custom-call(bf16[512,2560]{1,0:T(8,128)(2,1)} %get-tuple-element.63.u_ref, bf16[2,2560,5120]{2,1,0:T(8,128)(2,1)} %wg_ref.7, bf16[2,2560,5120]{2,1,0:T(8,128)(2,1)} %wu_ref.7, bf16[2,5120,2560]{2,1,0:T(8,128)(2,1)} %wd_ref.7), custom_call_target="tpu_custom_call" | custom-call | flops 40265318400 | bytes 83886080 | tf_op jit(solution)/shard_map/ffn/pallas_call | solution.py:362
  656.3 13.9 %wo.6 = (bf16[512,2560]{1,0:T(8,128)(2,1)}, bf16[512,2560]{1,0:T(8,128)(2,1)}) custom-call(s32[1]{0:T(128)} %bitcast.tp_ref, bf16[512,2560]{1,0:T(8,128)(2,1)} %get-tuple-element.45.x_ref, bf16[512,1024]{1,0:T(8,128)(2,1)} %merge.4.o0_ref, bf16[512,1024]{1,0:T(8,128)(2,1)} %collective-permute-done.15.o1_ref, bf16[2048,2560]{1,0:T(8,128)(2,1)} %bitcast.56, ...), custom_call_target="tpu_custom_call" | custom-call | flops 5368709120 | bytes 18350080 | tf_op jit(solution)/shard_map/wo/pallas_call | solution.py:321
  670.2 50.1 %ffn.6.d0_ref = bf16[512,2560]{1,0:T(8,128)(2,1)} custom-call(bf16[512,2560]{1,0:T(8,128)(2,1)} %get-tuple-element.60.u_ref, bf16[2,2560,5120]{2,1,0:T(8,128)(2,1)} %wg_ref.7, bf16[2,2560,5120]{2,1,0:T(8,128)(2,1)} %wu_ref.7, bf16[2,5120,2560]{2,1,0:T(8,128)(2,1)} %wd_ref.7), custom_call_target="tpu_custom_call" | custom-call | flops 40265318400 | bytes 83886080 | tf_op jit(solution)/shard_map/ffn/pallas_call | solution.py:362
  733.1 42.9 %collective-permute-done.16.d1_ref = bf16[512,2560]{1,0:T(8,128)(2,1)} collective-permute-done((bf16[512,2560]{1,0:T(8,128)(2,1)}, bf16[512,2560]{1,0:T(8,128)(2,1)}, u32[]{:S(2)}, u32[]{:S(2)}) %collective-permute-start.16) | collective-permute-done | bytes 2621472 | tf_op jit(solution)/shard_map/ppermute | solution.py:445
  (83 shorter events, 81.9 us)
Async XLA Ops:
  7.2 73.1 %all-gather.5.cloned.1.call-start = ((), (), s32[]{:S(2)}) async-start(), calls=%async_computation | async-start | bytes 11796480 | tf_op jit(solution)/shard_map/all_gather | solution.py:435
  7.2 7.8 copy-start.7
  10.7 562.6 %all-gather.7.cloned.1.call-start = ((), (), s32[]{:S(2)}) async-start(), calls=%async_computation.1 | async-start | bytes 11796480 | tf_op jit(solution)/shard_map/all_gather | solution.py:435
  35.0 9.9 %copy-start.4 = (bf16[1024,2,256]{2,1,0:T(2,128)(2,1)S(1)}, bf16[1024,2,256]{2,1,0:T(2,128)(2,1)}, u32[]{:S(2)}) copy-start(bf16[1024,2,256]{2,1,0:T(2,128)(2,1)} %param.20) | copy-start | bytes 3145732
  35.0 10.1 %collective-permute-start = (bf16[1024,512]{1,0:T(8,128)(2,1)}, bf16[1024,512]{1,0:T(8,128)(2,1)}, u32[]{:S(2)}, u32[]{:S(2)}) collective-permute-start(bf16[1024,512]{1,0:T(8,128)(2,1)} %get-tuple-element.36.ko_ref), channel_id=1, source_target_pairs={{0,1},{1,2},{2,3},{4,5},{5,6},{6,7}} | collective-permute-start | bytes 3145736 | tf_op jit(solution)/shard_map/ppermute | solution.py:455
  38.8 9.3 %collective-permute-start.1 = (bf16[1024,512]{1,0:T(8,128)(2,1)}, bf16[1024,512]{1,0:T(8,128)(2,1)}, u32[]{:S(2)}, u32[]{:S(2)}) collective-permute-start(bf16[1024,512]{1,0:T(8,128)(2,1)} %get-tuple-element.37.vo_ref), channel_id=1, source_target_pairs={{0,1},{1,2},{2,3},{4,5},{5,6},{6,7}} | collective-permute-start | bytes 3145736 | tf_op jit(solution)/shard_map/ppermute | solution.py:455
  59.9 20.4 %collective-permute-start.4 = (bf16[512,1024]{1,0:T(8,128)(2,1)}, bf16[512,1024]{1,0:T(8,128)(2,1)}, u32[]{:S(2)}, u32[]{:S(2)}) collective-permute-start(bf16[512,1024]{1,0:T(8,128)(2,1)} %window.3.o0_ref), channel_id=1, source_target_pairs={{0,4},{4,0},{1,5},{5,1},{2,6},{6,2},{3,7},{7,3}} | collective-permute-start | bytes 3145736 | tf_op jit(solution)/shard_map/ppermute | solution.py:439
  69.6 76.5 %collective-permute-start.2 = (bf16[512,1024]{1,0:T(8,128)(2,1)}, bf16[512,1024]{1,0:T(8,128)(2,1)}, u32[]{:S(2)}, u32[]{:S(2)}) collective-permute-start(bf16[512,1024]{1,0:T(8,128)(2,1)} %window.2.o0_ref), channel_id=1, source_target_pairs={{0,4},{4,0},{1,5},{5,1},{2,6},{6,2},{3,7},{7,3}} | collective-permute-start | bytes 3145736 | tf_op jit(solution)/shard_map/ppermute | solution.py:439
  144.4 69.4 %collective-permute-start.5 = (bf16[512,2560]{1,0:T(8,128)(2,1)}, bf16[512,2560]{1,0:T(8,128)(2,1)}, u32[]{:S(2)}, u32[]{:S(2)}) collective-permute-start(bf16[512,2560]{1,0:T(8,128)(2,1)} %ffn.5.refs_1_), channel_id=1, source_target_pairs={{0,4},{4,0},{1,5},{5,1},{2,6},{6,2},{3,7},{7,3}} | collective-permute-start | bytes 7864328 | tf_op jit(solution)/shard_map/ppermute | solution.py:445
  210.4 43.5 %collective-permute-start.3 = (bf16[512,2560]{1,0:T(8,128)(2,1)}, bf16[512,2560]{1,0:T(8,128)(2,1)}, u32[]{:S(2)}, u32[]{:S(2)}) collective-permute-start(bf16[512,2560]{1,0:T(8,128)(2,1)} %ffn.4.refs_1_), channel_id=1, source_target_pairs={{0,4},{4,0},{1,5},{5,1},{2,6},{6,2},{3,7},{7,3}} | collective-permute-start | bytes 7864328 | tf_op jit(solution)/shard_map/ppermute | solution.py:445
  269.4 77.9 %collective-permute-start.8 = (bf16[4,1024,256]{2,1,0:T(8,128)(2,1)}, bf16[4,1024,256]{2,1,0:T(8,128)(2,1)}, u32[]{:S(2)}, u32[]{:S(2)}) collective-permute-start(bf16[4,1024,256]{2,1,0:T(8,128)(2,1)} %get-tuple-element.46.q_ref), channel_id=1, source_target_pairs={{0,2},{1,3},{2,0},{3,1},{4,6},{5,7},{6,4},{7,5}} | collective-permute-start | bytes 6291464 | tf_op jit(solution)/shard_map/ppermute | solution.py:478
  307.6 39.8 %collective-permute-start.6 = (bf16[4,1024,256]{2,1,0:T(8,128)(2,1)}, bf16[4,1024,256]{2,1,0:T(8,128)(2,1)}, u32[]{:S(2)}, u32[]{:S(2)}) collective-permute-start(bf16[4,1024,256]{2,1,0:T(8,128)(2,1)} %get-tuple-element.46.q_ref), channel_id=1, source_target_pairs={{0,1},{1,0},{2,3},{3,2},{4,5},{5,4},{6,7},{7,6}} | collective-permute-start | bytes 6291464 | tf_op jit(solution)/shard_map/ppermute | solution.py:479
  347.4 50.7 %collective-permute-start.9 = (bf16[4,1024,256]{2,1,0:T(8,128)(2,1)}, bf16[4,1024,256]{2,1,0:T(8,128)(2,1)}, u32[]{:S(2)}, u32[]{:S(2)}) collective-permute-start(bf16[4,1024,256]{2,1,0:T(8,128)(2,1)} %collective-permute-done.8.q_ref), channel_id=1, source_target_pairs={{0,1},{1,0},{2,3},{3,2},{4,5},{5,4},{6,7},{7,6}} | collective-permute-start | bytes 6291464 | tf_op jit(solution)/shard_map/ppermute | solution.py:480
  397.6 162.7 %collective-permute-start.7 = (bf16[1024,1024]{1,0:T(8,128)(2,1)}, bf16[1024,1024]{1,0:T(8,128)(2,1)}, u32[]{:S(2)}, u32[]{:S(2)}) collective-permute-start(bf16[1024,1024]{1,0:T(8,128)(2,1)} %get-tuple-element.50), channel_id=1, source_target_pairs={{0,1},{1,0},{2,3},{3,2},{4,5},{5,4},{6,7},{7,6}} | collective-permute-start | bytes 6291464 | tf_op jit(solution)/shard_map/ppermute | solution.py:476
  397.6 162.7 %collective-permute-start.13 = (bf16[1024,128]{1,0:T(8,128)(2,1)}, bf16[1024,128]{1,0:T(8,128)(2,1)S(1)}, u32[]{:S(2)}, u32[]{:S(2)}) collective-permute-start(bf16[1024,128]{1,0:T(8,128)(2,1)} %get-tuple-element.57), channel_id=1, source_target_pairs={{0,1},{1,0},{2,3},{3,2},{4,5},{5,4},{6,7},{7,6}} | collective-permute-start | bytes 786440 | tf_op jit(solution)/shard_map/ppermute | solution.py:476
  448.7 50.7 %collective-permute-start.10 = (bf16[1024,1024]{1,0:T(8,128)(2,1)}, bf16[1024,1024]{1,0:T(8,128)(2,1)}, u32[]{:S(2)}, u32[]{:S(2)}) collective-permute-start(bf16[1024,1024]{1,0:T(8,128)(2,1)} %get-tuple-element.52), channel_id=1, source_target_pairs={{0,1},{1,0},{2,3},{3,2},{4,5},{5,4},{6,7},{7,6}} | collective-permute-start | bytes 6291464 | tf_op jit(solution)/shard_map/ppermute | solution.py:476
  448.7 50.7 %collective-permute-start.11 = (bf16[1024,128]{1,0:T(8,128)(2,1)}, bf16[1024,128]{1,0:T(8,128)(2,1)S(1)}, u32[]{:S(2)}, u32[]{:S(2)}) collective-permute-start(bf16[1024,128]{1,0:T(8,128)(2,1)} %get-tuple-element.54), channel_id=1, source_target_pairs={{0,1},{1,0},{2,3},{3,2},{4,5},{5,4},{6,7},{7,6}} | collective-permute-start | bytes 786440 | tf_op jit(solution)/shard_map/ppermute | solution.py:476
  507.1 53.3 %collective-permute-start.12 = (bf16[1024,1024]{1,0:T(8,128)(2,1)}, bf16[1024,1024]{1,0:T(8,128)(2,1)}, u32[]{:S(2)}, u32[]{:S(2)}) collective-permute-start(bf16[1024,1024]{1,0:T(8,128)(2,1)} %get-tuple-element.55), channel_id=1, source_target_pairs={{0,2},{1,3},{2,0},{3,1},{4,6},{5,7},{6,4},{7,5}} | collective-permute-start | bytes 6291464 | tf_op jit(solution)/shard_map/ppermute | solution.py:476
  507.1 53.2 %collective-permute-start.14 = (bf16[1024,128]{1,0:T(8,128)(2,1)}, bf16[1024,128]{1,0:T(8,128)(2,1)S(1)}, u32[]{:S(2)}, u32[]{:S(2)}) collective-permute-start(bf16[1024,128]{1,0:T(8,128)(2,1)} %get-tuple-element.58), channel_id=1, source_target_pairs={{0,2},{1,3},{2,0},{3,1},{4,6},{5,7},{6,4},{7,5}} | collective-permute-start | bytes 786440 | tf_op jit(solution)/shard_map/ppermute | solution.py:476
  566.2 26.0 %collective-permute-start.17 = (bf16[512,1024]{1,0:T(8,128)(2,1)}, bf16[512,1024]{1,0:T(8,128)(2,1)}, u32[]{:S(2)}, u32[]{:S(2)}) collective-permute-start(bf16[512,1024]{1,0:T(8,128)(2,1)} %merge.5.o0_ref), channel_id=1, source_target_pairs={{0,4},{4,0},{1,5},{5,1},{2,6},{6,2},{3,7},{7,3}} | collective-permute-start | bytes 3145736 | tf_op jit(solution)/shard_map/ppermute | solution.py:439
  571.5 84.8 %collective-permute-start.15 = (bf16[512,1024]{1,0:T(8,128)(2,1)}, bf16[512,1024]{1,0:T(8,128)(2,1)}, u32[]{:S(2)}, u32[]{:S(2)}) collective-permute-start(bf16[512,1024]{1,0:T(8,128)(2,1)} %merge.4.o0_ref), channel_id=1, source_target_pairs={{0,4},{4,0},{1,5},{5,1},{2,6},{6,2},{3,7},{7,3}} | collective-permute-start | bytes 3145736 | tf_op jit(solution)/shard_map/ppermute | solution.py:439
  656.0 71.5 %collective-permute-start.18 = (bf16[512,2560]{1,0:T(8,128)(2,1)}, bf16[512,2560]{1,0:T(8,128)(2,1)}, u32[]{:S(2)}, u32[]{:S(2)}) collective-permute-start(bf16[512,2560]{1,0:T(8,128)(2,1)} %ffn.7.d0_ref), channel_id=1, source_target_pairs={{0,4},{4,0},{1,5},{5,1},{2,6},{6,2},{3,7},{7,3}} | collective-permute-start | bytes 7864328 | tf_op jit(solution)/shard_map/ppermute | solution.py:445
  720.4 5.0 copy-start
  720.4 55.7 %collective-permute-start.16 = (bf16[512,2560]{1,0:T(8,128)(2,1)}, bf16[512,2560]{1,0:T(8,128)(2,1)}, u32[]{:S(2)}, u32[]{:S(2)}) collective-permute-start(bf16[512,2560]{1,0:T(8,128)(2,1)} %ffn.6.d0_ref), channel_id=1, source_target_pairs={{0,4},{4,0},{1,5},{5,1},{2,6},{6,2},{3,7},{7,3}} | collective-permute-start | bytes 7864328 | tf_op jit(solution)/shard_map/ppermute | solution.py:445
  (6 other events, 12.5 us)
Sparse Core Ops, SparseCore 0:
  10.8 69.3 all-gather.4
  82.0 100.5 all-gather.6

commit v2 on v1

v2 whole, which is shorter than its diff:
```python
import functools

import jax
import jax.numpy as jnp
from jax import lax
from jax.experimental import pallas as pl
from jax.experimental.pallas import tpu as pltpu
from jax.sharding import PartitionSpec as P

F32 = jnp.float32
BF16 = jnp.bfloat16
EPS = 1e-6
NEG = -1e30
LOG2E = 1.4426950408889634
HD = 256
VMEM_MAX = 63 * 2**20
ROW = ('arbitrary',)


def cost(flops, nbytes, trans=0):
    return pl.CostEstimate(flops=int(flops), bytes_accessed=int(nbytes), transcendentals=int(trans))


def params(n_axes):
    return pltpu.CompilerParams(dimension_semantics=('arbitrary',) * n_axes, vmem_limit_bytes=VMEM_MAX)


def rms(t, gain):
    return t * lax.rsqrt(jnp.mean(t * t, axis=-1, keepdims=True) + EPS) * (1.0 + gain)


def turn(t, gain, cos, sin):
    t = rms(t, gain)
    lo, hi = t[:, :HD // 2], t[:, HD // 2:]
    return jnp.concatenate([lo * cos - hi * sin, hi * cos + lo * sin], axis=1).astype(BF16)


def qkv_kernel(n_q, n_kv, x_ref, d0_ref, d1_ref, gd_ref, g_ref, qk_ref, wq_ref, wk_ref, wv_ref, cos_ref, sin_ref, q_ref, k_ref, v_ref, mid_ref):
    d = (d0_ref[...].astype(F32) + d1_ref[...].astype(F32)).astype(BF16).astype(F32)
    mid = (x_ref[...].astype(F32) + rms(d, gd_ref[...])).astype(BF16)
    mid_ref[...] = mid
    h = rms(mid.astype(F32), g_ref[...]).astype(BF16)
    cos, sin = cos_ref[...], sin_ref[...]
    kf = jnp.dot(h, wk_ref[0], preferred_element_type=F32)
    for n in range(n_kv):
        k_ref[:, n * HD:(n + 1) * HD] = turn(kf[:, n * HD:(n + 1) * HD], qk_ref[1:2, :], cos, sin)
    v_ref[...] = jnp.dot(h, wv_ref[0], preferred_element_type=F32).astype(BF16)
    qf = jnp.dot(h, wq_ref[0], preferred_element_type=F32)
    for n in range(n_q):
        q_ref[n] = turn(qf[:, n * HD:(n + 1) * HD], qk_ref[0:1, :], cos, sin)


def qkv(layer, x, d_pair, gd, gain, qk, wq, wk, wv, cos, sin, row0, tile=256):
    rows, dim = x.shape
    n_q, n_kv = wq.shape[2] // HD, wk.shape[2] // HD
    t0 = row0 // tile
    rowb = pl.BlockSpec((tile, dim), lambda i: (i, 0))
    vec = pl.BlockSpec((1, dim), lambda i: (0, 0))
    wspec = lambda w: pl.BlockSpec((1, dim, w.shape[2]), lambda i: (layer, 0, 0))
    trig = pl.BlockSpec((tile, HD // 2), lambda i: (i + t0, 0))
    kvb = pl.BlockSpec((tile, n_kv * HD), lambda i: (i, 0))
    cols = (n_q + 2 * n_kv) * HD
    return pl.pallas_call(
        functools.partial(qkv_kernel, n_q, n_kv), grid=(rows // tile,),
        in_specs=[rowb, rowb, rowb, vec, vec, pl.BlockSpec((2, HD), lambda i: (0, 0)), wspec(wq), wspec(wk), wspec(wv), trig, trig],
        out_specs=[pl.BlockSpec((n_q, tile, HD), lambda i: (0, i, 0)), kvb, kvb, rowb],
        out_shape=[jax.ShapeDtypeStruct((n_q, rows, HD), BF16)] + [jax.ShapeDtypeStruct((rows, n_kv * HD), BF16)] * 2 + [jax.ShapeDtypeStruct((rows, dim), BF16)],
        compiler_params=params(1),
        cost_estimate=cost(2 * rows * dim * cols, 2 * (rows * dim + dim * cols + rows * cols)), name='qkv')(x, *d_pair, gd, gain, qk, wq, wk, wv, cos, sin)


def kv_kernel(n_kv, steps, x_ref, g_ref, qk_ref, wk_ref, wv_ref, cos_ref, sin_ref, k0_ref, k1_ref, v0_ref, v1_ref, h_ref):
    i = pl.program_id(0)
    h = rms(x_ref[...].astype(F32), g_ref[...]).astype(BF16)
    h_ref[...] = h
    kf = jnp.dot(h, wk_ref[0], preferred_element_type=F32)
    k = jnp.concatenate([turn(kf[:, n * HD:(n + 1) * HD], qk_ref[1:2, :], cos_ref[...], sin_ref[...]) for n in range(n_kv)], axis=1)
    v = jnp.dot(h, wv_ref[0], preferred_element_type=F32).astype(BF16)

    @pl.when(i < steps // 2)
    def _():
        k0_ref[...] = k
        v0_ref[...] = v

    @pl.when(i >= steps // 2)
    def _():
        k1_ref[...] = k
        v1_ref[...] = v


def kv_first(layer, x, gain, qk, wk, wv, cos, sin, tile=256):
    rows, dim = x.shape
    cols = wk.shape[2]
    steps = rows // tile
    rowb = pl.BlockSpec((tile, dim), lambda i: (i, 0))
    wspec = pl.BlockSpec((1, dim, cols), lambda i: (layer, 0, 0))
    trig = pl.BlockSpec((tile, HD // 2), lambda i: (i, 0))
    lower = pl.BlockSpec((tile, cols), lambda i: (jnp.minimum(i, steps // 2 - 1), 0))
    upper = pl.BlockSpec((tile, cols), lambda i: (jnp.maximum(i - steps // 2, 0), 0))
    return pl.pallas_call(
        functools.partial(kv_kernel, cols // HD, steps), grid=(steps,),
        in_specs=[rowb, pl.BlockSpec((1, dim), lambda i: (0, 0)), pl.BlockSpec((2, HD), lambda i: (0, 0)), wspec, wspec, trig, trig],
        out_specs=[lower, upper, lower, upper, rowb],
        out_shape=[jax.ShapeDtypeStruct((rows // 2, cols), BF16)] * 4 + [jax.ShapeDtypeStruct((rows, dim), BF16)],
        compiler_params=params(1),
        cost_estimate=cost(4 * rows * dim * cols, 4 * (rows * dim + dim * cols + rows * cols)), name='kv')(x, gain, qk, wk, wv, cos, sin)


def q_kernel(n_q, h_ref, qk_ref, wq_ref, cos_ref, sin_ref, q_ref):
    qf = jnp.dot(h_ref[...], wq_ref[0], preferred_element_type=F32)
    for n in range(n_q):
        q_ref[n] = turn(qf[:, n * HD:(n + 1) * HD], qk_ref[0:1, :], cos_ref[...], sin_ref[...])


def q_after(layer, h, qk, wq, cos, sin, tile=512):
    rows, dim = h.shape
    n_q = wq.shape[2] // HD
    trig = pl.BlockSpec((tile, HD // 2), lambda i: (i, 0))
    return pl.pallas_call(
        functools.partial(q_kernel, n_q), grid=(rows // tile,),
        in_specs=[pl.BlockSpec((tile, dim), lambda i: (i, 0)), pl.BlockSpec((2, HD), lambda i: (0, 0)), pl.BlockSpec((1, dim, n_q * HD), lambda i: (layer, 0, 0)), trig, trig],
        out_specs=pl.BlockSpec((n_q, tile, HD), lambda i: (0, i, 0)),
        out_shape=jax.ShapeDtypeStruct((n_q, rows, HD), BF16), compiler_params=params(1),
        cost_estimate=cost(2 * rows * dim * n_q * HD, 2 * (rows + n_q * HD) * dim), name='q')(h, qk, wq, cos, sin)


def window_kernel(tile, tiles, halves, flag_ref, q_ref, *refs):
    n = len(halves)
    gots, caches, owns = refs[:2 * n], refs[2 * n:4 * n], refs[4 * n:4 * n + 4]
    o_ref = refs[4 * n + 4]
    prevs = refs[4 * n + 5:]
    first = flag_ref[0] == 0
    for p, g, c in zip(prevs, gots, caches):
        p[...] = jnp.where(first, c[...], g[...])
    scale = LOG2E * HD ** -0.5
    rows2 = 2 * tile
    row = lax.broadcasted_iota(jnp.int32, (rows2, tile), 0) & (tile - 1)
    col = lax.broadcasted_iota(jnp.int32, (rows2, tile), 1)
    each = owns[0].shape[0]
    nb = 2 * each // tile
    for j, t in enumerate(tiles):
        q = q_ref[:, t * tile:(t + 1) * tile, :].reshape(rows2, HD)
        pieces = []
        for b in range(t, t + nb + 1):
            half, st = divmod(b % nb * tile, each)
            kr, vr = (prevs[halves.index(half)], prevs[n + halves.index(half)]) if b < nb else (owns[half], owns[2 + half])
            pieces.append((kr, vr, st))
        ss = []
        for i, (kr, _, st) in enumerate(pieces):
            s = lax.dot_general(q, kr[st:st + tile, :], (((1,), (1,)), ((), ())), preferred_element_type=F32) * scale
            if i == 0:
                s = jnp.where(col > row, s, NEG)
            if i == nb:
                s = jnp.where(col <= row, s, NEG)
            ss.append(s)
        top = ss[0]
        for s in ss[1:]:
            top = jnp.maximum(top, s)
        top = top.max(axis=1, keepdims=True)
        total = jnp.zeros((rows2, tile), F32)
        acc = jnp.zeros((rows2, HD), F32)
        for s, (_, vr, st) in zip(ss, pieces):
            p = jnp.exp2(s - top)
            total = total + p
            acc = acc + jnp.dot(p.astype(BF16), vr[st:st + tile, :], preferred_element_type=F32)
        out = (acc / total.sum(axis=1, keepdims=True)).astype(BF16)
        for g in range(2):
            o_ref[j * tile:(j + 1) * tile, g * HD:(g + 1) * HD] = out[g * tile:(g + 1) * tile]


def window_attention(flag, q, got, cache, own, halves, row0, rows, tile=256):
    n_q, total, _ = q.shape
    n_kv = n_q // 2
    part = own[0].shape[0]
    tiles = tuple(range(row0 // tile, (row0 + rows) // tile))
    kv = lambda i: pl.BlockSpec((part, HD), lambda h, *_: (i, h))
    ins = [got[i][j] for j in range(2) for i in halves] + [cache[j] for j in range(2) for _ in halves] + list(own)
    specs = [kv(0)] * (2 * len(halves)) + [kv(i) for _ in range(2) for i in halves] + [kv(0)] * 4
    return pl.pallas_call(
        functools.partial(window_kernel, tile, tiles, tuple(halves)),
        grid_spec=pltpu.PrefetchScalarGridSpec(
            num_scalar_prefetch=1, grid=(n_kv,),
            in_specs=[pl.BlockSpec((2, total, HD), lambda h, *_: (h, 0, 0))] + specs,
            out_specs=pl.BlockSpec((rows, 2 * HD), lambda h, *_: (0, h)),
            scratch_shapes=[pltpu.VMEM((part, HD), BF16)] * (2 * len(halves))),
        out_shape=jax.ShapeDtypeStruct((rows, n_q * HD), BF16), compiler_params=params(1),
        cost_estimate=cost(4 * rows * n_q * (2 * part + tile) * HD, 2 * (4 * total * n_kv * HD + 2 * rows * n_q * HD)), name='window')(flag, q, *ins)


def split3(x):
    hi = x.astype(BF16)
    r = x - hi.astype(F32)
    mid = r.astype(BF16)
    return hi, mid, (r - mid.astype(F32)).astype(BF16)


def global_kernel(offsets, own, n_parts, bq, bk, use_cache, use_new, want_aux, *refs):
    halves = len(offsets)
    sc_ref, norm_ref, refs = refs[0], refs[1], refs[2:]
    qs, refs = refs[:halves], refs[halves:]
    if use_cache:
        (kc_ref, vc_ref), refs = refs[:2], refs[2:]
    if use_new:
        news, refs = refs[:4], refs[4:]
    parts, refs = refs[:2 * n_parts * halves], refs[2 * n_parts * halves:]
    per = 2 if want_aux else 1
    outs, refs = refs[:per * halves], refs[per * halves:]
    m_ref, l_ref, acc_ref = refs[:3]
    head = pl.program_id(0)
    scale = LOG2E * HD ** -0.5
    small = 256
    chains = [(hf, g) for hf in range(halves) for g in range(2)]
    rows_of = lambda hf, g: slice((2 * hf + g) * bq, (2 * hf + g + 1) * bq)
    l_ref[...] = jnp.zeros_like(l_ref)
    acc_ref[...] = jnp.zeros_like(acc_ref)
    if use_new:
        kn_ref, vn_ref = refs[3:5]
        half = news[0].shape[0]
        for i in range(2):
            kn_ref[i * half:(i + 1) * half, :] = news[i][...]
            vn_ref[i * half:(i + 1) * half, :] = news[2 + i][...]
    later = jnp.where(sc_ref[1] > 0, 1, 0) if use_new and not own else 0
    n_valid = sc_ref[0]

    def dot_qk(hf, g, k):
        return lax.dot_general(qs[hf][g], k, (((1,), (1,)), ((), ())), preferred_element_type=F32)

    worst = jnp.full((1, 1), NEG, F32)
    for hf, g in chains:
        k = kc_ref[:small, :] if use_cache else kn_ref[:small, :]
        m = dot_qk(hf, g, k).max(axis=1, keepdims=True) * scale
        m_ref[rows_of(hf, g), :] = jnp.broadcast_to(m, (bq, 128))
        qf = qs[hf][g].astype(F32)
        size = jnp.sqrt((qf * qf).sum(axis=1, keepdims=True))
        worst = jnp.maximum(worst, (size * (norm_ref[head] * scale) - m).max(axis=0, keepdims=True))
    steady = worst[0, 0] <= 60.0

    def steady_block(live, k, v, mask):
        for hf, g in live:
            rows = rows_of(hf, g)
            s = dot_qk(hf, g, k)
            if mask is not None:
                s = jnp.where(mask, s, NEG)
            m = m_ref[rows, :]
            l = l_ref[rows, :]
            ps = []
            for j in range(k.shape[0] // 128):
                p = jnp.exp2(s[:, j * 128:(j + 1) * 128] * scale - m)
                l = l + p
                ps.append(p.astype(BF16))
            l_ref[rows, :] = l
            acc_ref[rows, :] += jnp.dot(jnp.concatenate(ps, axis=1), v, preferred_element_type=F32)

    def online_block(live, k, v, mask):
        for hf, g in live:
            rows = rows_of(hf, g)
            s = dot_qk(hf, g, k)
            if mask is not None:
                s = jnp.where(mask, s, NEG)
            m_prev = m_ref[rows, :]
            m_new = jnp.maximum(m_prev, s.max(axis=1, keepdims=True) * scale)
            alpha = jnp.exp2(m_prev - m_new)
            p = jnp.exp2(s * scale - m_new[:, :1])
            l_ref[rows, :] = l_ref[rows, :] * alpha + p.sum(axis=1, keepdims=True) * (1.0 / 128)
            m_ref[rows, :] = m_new
            acc_ref[rows, :] = acc_ref[rows, :] * alpha[:, :1] + jnp.dot(p.astype(BF16), v, preferred_element_type=F32)

    def run(block, size):
        joined = use_new and not own and size == 2 * half if use_new else False
        at = lambda i, n: pl.ds(pl.multiple_of(i * n, n), n)
        if use_cache:
            n_full = n_valid // size
            last_block = kc_ref.shape[0] // size - 1

            def step(i, c):
                sl = at(jnp.minimum(i, last_block), size)
                k, v = kc_ref[sl, :], vc_ref[sl, :]
                if joined:
                    k = jnp.where(i >= n_full, kn_ref[...], k)
                    v = jnp.where(i >= n_full, vn_ref[...], v)
                block(chains, k, v, None)
                return c

            lax.fori_loop(0, n_full + (later if joined else 0), step, 0)

            def edge(i, c):
                sl = at(i, small)
                block(chains, kc_ref[sl, :], vc_ref[sl, :], (i * small + lax.broadcasted_iota(jnp.int32, (bq, small), 1)) < n_valid)
                return c

            lax.fori_loop(n_full * (size // small), (n_valid + small - 1) // small, edge, 0)
        if use_new and not own and not (joined and use_cache):
            def new_step(i, c):
                sl = at(i, size)
                block(chains, kn_ref[sl, :], vn_ref[sl, :], None)
                return c

            lax.fori_loop(0, later * (2 * half // size), new_step, 0)
        if own:
            for hf, off in enumerate(offsets):
                live = [(hf, g) for g in range(2)]
                if off:
                    block(live, kn_ref[:off, :], vn_ref[:off, :], None)
                causal = lax.broadcasted_iota(jnp.int32, (bq, bq), 1) <= lax.broadcasted_iota(jnp.int32, (bq, bq), 0)
                block(live, kn_ref[off:off + bq, :], vn_ref[off:off + bq, :], causal)

    @pl.when(steady)
    def _():
        run(steady_block, bk)

    @pl.when(jnp.logical_not(steady))
    def _():
        m_ref[...] = jnp.full_like(m_ref, NEG)
        run(online_block, small)

    lane = lax.broadcasted_iota(jnp.int32, (bq, 128), 1)
    for hf, g in chains:
        c = 2 * hf + g
        rows = slice(c * bq, (c + 1) * bq)
        cs = slice(g * HD, (g + 1) * HD)
        first = 16 * (2 * head + g)
        l = l_ref[rows, :].sum(axis=1, keepdims=True)
        m = jnp.where(l > 0.0, m_ref[rows, 0:1], NEG)
        mine = parts[2 * n_parts * hf:2 * n_parts * (hf + 1)]
        lses = [jnp.where((lane >= first) & (lane < first + 3), a[...].astype(F32), 0.0).sum(axis=1, keepdims=True) for a in mine[1::2]]
        top = functools.reduce(jnp.maximum, lses, m)
        w0 = jnp.exp2(m - top)
        ws = [jnp.exp2(s - top) for s in lses]
        total = functools.reduce(jnp.add, ws, l * w0)
        o = acc_ref[rows, :] * w0
        for p, w in zip(mine[0::2], ws):
            o = o + p[:, cs].astype(F32) * w
        outs[per * hf][:, cs] = (o / total).astype(BF16)
        if want_aux:
            aux_ref = outs[per * hf + 1]
            lse = jnp.broadcast_to(top + jnp.log2(total), (bq, 128))
            aux = aux_ref[...]
            for p, part in enumerate(split3(lse)):
                aux = jnp.where(lane == first + p, part, aux)
            aux_ref[...] = aux


def global_attention(q_list, offsets, own, cache, new, sc, norms, parts, want_aux, bk=1024):
    n_q, bq, _ = q_list[0].shape
    halves = len(q_list)
    n_kv = n_q // 2
    n_parts = len(parts[0])
    kv = lambda a: pl.BlockSpec((a.shape[0], HD), lambda h, *_: (0, h))
    ob = pl.BlockSpec((bq, 2 * HD), lambda h, *_: (0, h))
    ab = pl.BlockSpec((bq, 128), lambda h, *_: (0, 0))
    ins = list(q_list)
    specs = [pl.BlockSpec((2, bq, HD), lambda h, *_: (h, 0, 0))] * halves
    keys = 0
    for group in (cache, new):
        if group is not None:
            ins += list(group)
            specs += [kv(a) for a in group]
            keys += sum(a.shape[0] for a in group) // 2
    for half_parts in parts:
        for o, aux in half_parts:
            ins += [o, aux]
            specs += [ob, ab]
    shapes, out_specs = [], []
    for _ in range(halves):
        shapes.append(jax.ShapeDtypeStruct((bq, n_q * HD), BF16))
        out_specs.append(ob)
        if want_aux:
            shapes.append(jax.ShapeDtypeStruct((bq, 128), BF16))
            out_specs.append(ab)
    m = 2 * halves * bq
    scratch = [pltpu.VMEM((m, 128), F32), pltpu.VMEM((m, 128), F32), pltpu.VMEM((m, HD), F32)]
    if new is not None:
        scratch += [pltpu.VMEM((2 * new[0].shape[0], HD), BF16)] * 2
    rows = halves * bq
    outs = pl.pallas_call(
        functools.partial(global_kernel, tuple(offsets), own, n_parts, bq, bk, cache is not None, new is not None, want_aux),
        grid_spec=pltpu.PrefetchScalarGridSpec(
            num_scalar_prefetch=2, grid=(n_kv,), in_specs=specs, out_specs=out_specs, scratch_shapes=scratch),
        out_shape=shapes, compiler_params=params(1),
        cost_estimate=cost(4 * rows * n_q * keys * HD, 2 * (2 * keys * n_kv * HD + 2 * rows * n_q * HD), rows * n_q * keys),
        name='gattn')(sc, norms, *ins)
    per = 2 if want_aux else 1
    return [tuple(outs[i * per:(i + 1) * per]) for i in range(halves)]


def wo_kernel(at_ref, x_ref, o0_ref, o1_ref, w_ref, near_ref, far_ref, ga_ref, gu_ref, x1_ref, u_ref, all_ref):
    tp, core = at_ref[0], at_ref[1]
    half = w_ref.shape[1]
    piece = near_ref.shape[0]

    @pl.when(pl.program_id(0) == 0)
    def _():
        all_ref[pl.ds(pl.multiple_of(tp * half, half), half), :] = w_ref[0]
        base = (1 - tp) * half
        all_ref[pl.ds(pl.multiple_of(base + core * piece, piece), piece), :] = near_ref[...]
        all_ref[pl.ds(pl.multiple_of(base + (1 - core) * piece, piece), piece), :] = far_ref[...]

    own, other = o0_ref[...], o1_ref[...]
    o = jnp.concatenate([jnp.where(tp == 0, own, other), jnp.where(tp == 0, other, own)], axis=1)
    a = jnp.dot(o, all_ref[...], preferred_element_type=F32).astype(BF16).astype(F32)
    x1 = (x_ref[...].astype(F32) + rms(a, ga_ref[...])).astype(BF16)
    x1_ref[...] = x1
    u_ref[...] = rms(x1.astype(F32), gu_ref[...]).astype(BF16)


def out_proj(layer, at, x, o_own, o_other, w, pieces, ga, gu, row0, tile=256):
    rows, half = o_own.shape
    dim = w.shape[2]
    t0 = row0 // tile
    rowb = pl.BlockSpec((tile, dim), lambda i, *_: (i, 0))
    vec = pl.BlockSpec((1, dim), lambda i, *_: (0, 0))
    ob = pl.BlockSpec((tile, half), lambda i, *_: (i, 0))
    pb = pl.BlockSpec(pieces[0].shape, lambda i, *_: (0, 0))
    return pl.pallas_call(
        wo_kernel,
        grid_spec=pltpu.PrefetchScalarGridSpec(
            num_scalar_prefetch=1, grid=(rows // tile,),
            in_specs=[pl.BlockSpec((tile, dim), lambda i, *_: (i + t0, 0)), ob, ob, pl.BlockSpec((1, half, dim), lambda i, *_: (layer, 0, 0)), pb, pb, vec, vec],
            out_specs=[rowb, rowb], scratch_shapes=[pltpu.VMEM((2 * half, dim), BF16)]),
        out_shape=[jax.ShapeDtypeStruct((rows, dim), BF16)] * 2, compiler_params=params(1),
        cost_estimate=cost(4 * rows * half * dim, 2 * (2 * half * dim + 3 * rows * dim)), name='wo')(at, x, o_own, o_other, w, *pieces, ga, gu)


def ffn_kernel(nb, u_ref, wg_ref, wu_ref, wd_ref, d_ref, act_ref, acc_ref):
    n = pl.program_id(0)

    def head(slot):
        g = jnp.dot(u_ref[...], wg_ref[0], preferred_element_type=F32)
        up = jnp.dot(u_ref[...], wu_ref[0], preferred_element_type=F32)
        act_ref[slot] = (jax.nn.gelu(g, approximate=True) * up).astype(BF16)

    def tail(slot):
        return jnp.dot(act_ref[slot], wd_ref[0], preferred_element_type=F32)

    @pl.when(n == 0)
    def _():
        head(0)
        acc_ref[...] = jnp.zeros_like(acc_ref)

    for slot in range(2):
        @pl.when((n > 0) & (n < nb) & (n % 2 == slot))
        def _():
            acc_ref[...] += tail(1 - slot)
            head(slot)

    @pl.when(n == nb)
    def _():
        d_ref[...] = (acc_ref[...] + tail((nb - 1) % 2)).astype(BF16)


def ffn(layer, u, wg, wu, wd, bn=512):
    rows, dim = u.shape
    width = wg.shape[2]
    nb = width // bn
    return pl.pallas_call(
        functools.partial(ffn_kernel, nb), grid=(nb + 1,),
        in_specs=[pl.BlockSpec((rows, dim), lambda n: (0, 0)),
                  pl.BlockSpec((1, dim, bn), lambda n: (layer, 0, jnp.minimum(n, nb - 1))),
                  pl.BlockSpec((1, dim, bn), lambda n: (layer, 0, jnp.minimum(n, nb - 1))),
                  pl.BlockSpec((1, bn, dim), lambda n: (layer, jnp.maximum(n - 1, 0), 0))],
        out_specs=pl.BlockSpec((rows, dim), lambda n: (0, 0)),
        out_shape=jax.ShapeDtypeStruct((rows, dim), BF16),
        scratch_shapes=[pltpu.VMEM((2, rows, bn), BF16), pltpu.VMEM((rows, dim), F32)],
        compiler_params=params(1),
        cost_estimate=cost(6 * rows * dim * width, 2 * (3 * dim * width + 2 * rows * dim), rows * width), name='ffn')(u, wg, wu, wd)


def last_kernel(x_ref, d0_ref, d1_ref, g_ref, *rest):
    d = (d0_ref[...].astype(F32) + d1_ref[...].astype(F32)).astype(BF16).astype(F32)
    rest[-1][...] = (x_ref[...].astype(F32) + rms(d, g_ref[...])).astype(BF16)


def last(x, d_pair, gain, total_rows, row0, carried, tile=256):
    rows, dim = x.shape
    t0 = row0 // tile
    rowb = pl.BlockSpec((tile, dim), lambda i: (i, 0))
    ins = [x, d_pair[0], d_pair[1], gain]
    specs = [rowb, rowb, rowb, pl.BlockSpec((1, dim), lambda i: (0, 0))]
    aliases = {}
    if carried is not None:
        aliases[4] = 0
        ins.append(carried)
        specs.append(pl.BlockSpec(memory_space=pl.ANY))
    return pl.pallas_call(
        last_kernel, grid=(rows // tile,), in_specs=specs,
        out_specs=pl.BlockSpec((tile, dim), lambda i: (i + t0, 0)),
        out_shape=jax.ShapeDtypeStruct((total_rows, dim), BF16), input_output_aliases=aliases,
        compiler_params=params(1), cost_estimate=cost(10 * rows * dim, 8 * rows * dim), name='last')(*ins)


def rope_tables(positions, base, divisor):
    inv_freq = 1.0 / (base ** (jnp.arange(0, HD, 2, dtype=F32) / HD))
    angles = (positions.astype(F32) / divisor)[:, None] * inv_freq[None, :]
    return jnp.cos(angles), jnp.sin(angles)


def solution(mesh):
    cp_size = mesh.shape['cp']
    tp_size = mesh.shape['tp']
    row_spec = P(('dp', 'cp'), None)
    cache_spec = P(('dp', 'cp'), 'tp', None)
    window_spec = P('dp', 'tp', None)
    col_spec = P(None, None, 'tp')
    row_split = P(None, 'tp', None)
    replicated = P()

    def device_step(hidden, start_pos, k_local, v_local, k_global, v_global, w_query, w_key, w_value, w_out, w_gate, w_up, w_down, norm_gain, qk_gain):
        first_pos = start_pos[0]
        cp_index = lax.axis_index('cp')
        tp_index = lax.axis_index('tp')
        core = jnp.remainder(cp_index, 2)
        at = jnp.stack([tp_index, core]).astype(jnp.int32)
        rows = hidden.shape[0]
        part = rows // 2
        n_kv = k_local.shape[1]
        shard_len = k_global.shape[0]
        positions = first_pos + cp_index * rows + jnp.arange(rows)
        gains = lambda l, i: norm_gain[l, i][None, :]
        move = lambda a, k: lax.ppermute(a, 'cp', [(i, i ^ k) for i in range(cp_size)])
        swap = lambda a: lax.ppermute(a, 'tp', [(i, tp_size - 1 - i) for i in range(tp_size)])
        after = lambda a, dep: lax.optimization_barrier((a, dep))[0]

        def out_weights(l, src):
            n = src.shape[1] // 2
            return swap(lax.dynamic_slice(src, (l, core * n, 0), (1, n, src.shape[2]))[0])

        def both_pieces(mine, dep):
            mine = after(mine, dep)
            return mine, move(mine, 1)

        def finish(l, i, x, row0, o, pieces):
            x1, u = out_proj(l, at, x, o, swap(o), w_out, pieces, gains(l, 1), gains(l, 2), row0)
            d = ffn(l, u, w_gate, w_up, w_down)
            return x1, (d, swap(d))

        piece = out_weights(0, w_out)
        cos, sin = rope_tables(positions, 10000.0, 1.0)
        k0, k1, v0, v1, h = kv_first(0, hidden, gains(0, 0), qk_gain[0], w_key, w_value, cos, sin)
        ahead = [(i, i + 1) for i in range(cp_size - 1)]
        pass_on = lambda a: lax.ppermute(a, 'cp', ahead)
        got = {1: (pass_on(k1), pass_on(v1)), 0: (pass_on(k0), pass_on(v0))}
        got[1], got[0] = lax.optimization_barrier((got[1], got[0]))
        shift = jnp.remainder(first_pos, k_local.shape[0])
        rolled = [jnp.roll(c.reshape(c.shape[0], -1), -shift, axis=0) for c in (k_local, v_local)]
        q = q_after(0, h, qk_gain[0], w_query, cos, sin)
        flag = cp_index.astype(jnp.int32)[None]
        xs, ds, os = {}, {}, {}
        own = (k0, k1, v0, v1)
        os[1] = window_attention(flag, q, got, rolled, own, (1,), part, part)
        os[0] = window_attention(after(flag, os[1]), q, got, rolled, own, (0, 1), 0, part)
        pieces = both_pieces(piece, os[0])
        for i in (1, 0):
            xs[i], ds[i] = finish(0, i, hidden, i * part, os[i], pieces)

        cos, sin = rope_tables(positions, 1000000.0, 8.0)
        q, k_new, v_new, mids = {}, {}, {}, {}
        def project(i, x):
            q[i], k_new[i], v_new[i], mids[i] = qkv(1, x, ds[i], gains(0, 3), gains(1, 0), qk_gain[1], w_query, w_key, w_value, cos, sin, i * part)

        project(1, xs[1])
        cache = [c.reshape(shard_len, -1) for c in (k_global, v_global)]
        n_valid = jnp.clip(first_pos - cp_index * shard_len, 0, shard_len)
        new = []
        widest = lambda a, live: jnp.sqrt(jnp.where(live[:, None], jnp.sum(jnp.square(a.astype(F32)), axis=-1), 0.0).max(axis=0))
        norms = {False: widest(k_global, jnp.arange(shard_len) < n_valid)}

        def attend(qh, owner, halves, parts, want_aux, use_cache=True, use_new=True):
            sc = jnp.stack([n_valid, (owner - cp_index) * rows]).astype(jnp.int32)
            return global_attention([qh[i] for i in halves], [i * part for i in halves], owner is cp_index, cache if use_cache else None, new if use_new else None, sc, norms[use_new], parts, want_aux)

        send = lambda pair, k: tuple(move(a, k) for a in pair)
        q1, q2, q3 = {}, {}, {}

        def spread(i):
            q1[i], q2[i] = move(q[i], 1), move(q[i], 2)

        spread(1)
        q3[1] = move(q2[1], 1)
        o1, o2, o3, own = {}, {}, {}, {}
        early, = attend(q1, cp_index ^ 1, (1,), [[]], True, use_new=False)
        project(0, after(xs[0], (early[0], q2[1])))
        new += [k_new[0], k_new[1], v_new[0], v_new[1]]
        norms[True] = functools.reduce(jnp.maximum, [widest(k_new[i].reshape(part, n_kv, HD), jnp.full((part,), True)) for i in (0, 1)], norms[False])
        spread(0)
        o1[0], = attend(q1, cp_index ^ 1, (0,), [[]], True)
        q2[0] = after(q2[0], o1[0][0])
        q3[0] = move(q2[0], 1)
        o2[0], o2[1] = attend(q2, cp_index ^ 2, (0, 1), [[], []], True)
        got2 = {i: send(o2[i], 1) for i in (0, 1)}
        q1[1] = after(q1[1], o2[0][0])
        o1[1], = attend(q1, cp_index ^ 1, (1,), [[early]], True, use_cache=False)
        q3[0] = after(q3[0], o1[1][0])
        o3[0], = attend(q3, cp_index ^ 3, (0,), [[got2[0]]], True)
        q3[1] = after(q3[1], o3[0][0])
        o3[1], = attend(q3, cp_index ^ 3, (1,), [[got2[1]]], True)
        pieces = both_pieces(out_weights(1, after(w_out, o1[0][0])), o3[0][0])
        got1 = {i: send(o1[i], 1) for i in (0, 1)}
        got3 = {i: send(o3[i], 3) for i in (0, 1)}
        q[0] = after(q[0], o3[1][0])
        (own[0],), = attend(q, cp_index, (0,), [[got1[0], got3[0]]], False)
        q[1] = after(q[1], own[0])
        (own[1],), = attend(q, cp_index, (1,), [[got1[1], got3[1]]], False)
        out = None
        for i in (0, 1):
            xs[i], ds[i] = finish(1, i, mids[i], 0, own[i], pieces)
        for i in (0, 1):
            out = last(xs[i], ds[i], gains(1, 3), rows, i * part, out)
        heads = lambda a: a.reshape(rows, n_kv, HD)
        join = lambda a, b: heads(jnp.concatenate([a, b], axis=0))
        return out, join(k0, k1), join(v0, v1), join(k_new[0], k_new[1]), join(v_new[0], v_new[1])

    return jax.shard_map(device_step, mesh=mesh, in_specs=(row_spec, P('dp'), window_spec, window_spec, cache_spec, cache_spec, col_spec, col_spec, col_spec, row_split, col_spec, col_spec, row_split, replicated, replicated), out_specs=(row_spec, cache_spec, cache_spec, cache_spec, cache_spec), check_vma=False)
```

time: 796 us -> 730 us (0.917)
  waiting for transfers between devices: 121 us -> 65.9 us
  starting transfers between devices: 57.8 us -> 31.9 us
  other arithmetic: 14.7 us -> 33.2 us
  between operations: 15.3 us -> 1.97 us
  Pallas kernels: 554 us -> 567 us
    ppermute x19 -> x34, waiting for transfers between devices: 121 us -> 65.9 us  [the longest x10 65.7 us: device_step(): lax.ppermute(a, 'tp', [(i, tp_size - 1 - i) for i in range(tp_size)])]
    ppermute x19 -> x34, starting transfers between devices: 57.7 us -> 31.9 us  [the longest x10 12 us: device_step(): lax.ppermute(a, 'tp', [(i, tp_size - 1 - i) for i in range(tp_size)])]
    reduce_sum x0 -> x3, other arithmetic: none -> 14 us  [device_step(): jnp.sum(jnp.square(a.astype(F32)), axis=-1)]
    pallas_call x12 -> x14, Pallas kernels: 287 us -> 294 us  [the longest x8 223 us: global_attention(): pl.pallas_call(functools.partial(global_kernel, tuple(offsets), own, n_pa...]
    unnamed x22 -> x50, local copies, waits for them, and re-layouts: 16.1 us -> 10.1 us
  transfers between devices with their start and end apart: 21 -> 34, of which waited for: 5 -> 3; matrix products, arithmetic and copies ran while one was open for 5% -> 7% of each run, Pallas kernels for 70% -> 75%
where the time goes in v2:
time: 730 us; the launch traced here: 725 us
  Pallas kernels  567 us (78%)
  waiting for transfers between devices  65.9 us (9%)
  other arithmetic  33.2 us (5%)
  starting transfers between devices  31.9 us (4%)
  local copies, waits for them, and re-layouts  24.8 us (3%)
    pallas_call x8, Pallas kernels, global_attention(): pl.pallas_call(functools.partial(global_kernel, tuple(offsets), own, n_pa...  223 us
    pallas_call x4, Pallas kernels, ffn(): pl.pallas_call(functools.partial(ffn_kernel, nb), grid=(nb + 1,), in_spec...  200 us
    ppermute x10, waiting for transfers between devices, device_step(): lax.ppermute(a, 'tp', [(i, tp_size - 1 - i) for i in range(tp_size)])  65.7 us
    pallas_call x4, Pallas kernels, out_proj(): pl.pallas_call(wo_kernel, grid_spec=pltpu.PrefetchScalarGridSpec(num_scal...  61.7 us
    pallas_call x2, Pallas kernels, qkv(): pl.pallas_call(functools.partial(qkv_kernel, n_q, n_kv), grid=(rows // ti...  31.1 us
    pallas_call x2, Pallas kernels, window_attention(): pl.pallas_call(functools.partial(window_kernel, tile, tiles, tuple(halves...  16.7 us
  transfers between devices with their start and end apart: 34, of which 3 were waited for; matrix products, arithmetic and copies ran while one was open for 7% of the time, Pallas kernels for 75%

profile of v2, /device:TPU:0, one launch (start us, length us, event | category | flops | bytes accessed | tf_op | source)
XLA Modules:
  0.0 724.9 jit_solution(13617747674434974952)
XLA Ops:
  12.5 12.5 %kv.1 = (bf16[512,512]{1,0:T(8,128)(2,1)}, bf16[512,512]{1,0:T(8,128)(2,1)}, bf16[512,512]{1,0:T(8,128)(2,1)}, bf16[512,512]{1,0:T(8,128)(2,1)}, bf16[1024,2560]{1,0:T(8,128)(2,1)}) custom-call(bf16[1024,2560]{1,0:T(8,128)(2,1)} %x_ref.5, f32[1,2560]{1,0:T(1,128)} %get-tuple-element.112.g_ref, f32[2,256]{1,0:T(2,128)} %get-tuple-element.119.qk_ref, ...), custom_call_target="tpu_custom_call" | custom-call | flops 5368709120 | bytes 17825792 | tf_op jit(solution)/shard_map/kv/pallas_call | solution.py:100
  41.2 11.2 %q.1.q_ref = bf16[4,1024,256]{2,1,0:T(8,128)(2,1)} custom-call(bf16[1024,2560]{1,0:T(8,128)(2,1)} %get-tuple-element.56.h_ref, f32[2,256]{1,0:T(2,128)} %get-tuple-element.119.qk_ref, bf16[2,2560,1024]{2,1,0:T(8,128)(2,1)} %wq_ref.5, f32[1024,128]{1,0:T(8,128)} %get-tuple-element.117.cos_ref, f32[1024,128]{1,0:T(8,128)} %get-tuple-element.116.sin_ref), custom_call_target="tpu_custom_call" | custom-call | flops 5368709120 | bytes 10485760 | tf_op jit(solution)/shard_map/q/pallas_call | solution.py:119
  60.6 8.5 %window.3.o0_ref = bf16[512,1024]{1,0:T(8,128)(2,1)} custom-call(s32[1]{0:T(128)} %bitcast.2.flag_ref, bf16[4,1024,256]{2,1,0:T(8,128)(2,1)} %q.1.q_ref, bf16[512,512]{1,0:T(8,128)(2,1)} %collective-permute-done.2.refs_0_, bf16[512,512]{1,0:T(8,128)(2,1)} %collective-permute-done.refs_0_.refs_1_, bf16[512,512]{1,0:T(8,128)(2,1)} %collective-permute-done.3.refs_2_, ...), custom_call_target="tpu_custom_call" | custom-call | flops 2684354560 | bytes 6291456 | tf_op jit(solution)/shard_map/window/pallas_call | solution.py:179
  75.0 20.2 %collective-permute-done.4.o1_ref = bf16[512,1024]{1,0:T(8,128)(2,1)} collective-permute-done((bf16[512,1024]{1,0:T(8,128)(2,1)}, bf16[512,1024]{1,0:T(8,128)(2,1)}, u32[]{:S(2)}, u32[]{:S(2)}) %collective-permute-start.4) | collective-permute-done | bytes 1048608 | tf_op jit(solution)/shard_map/ppermute | solution.py:520
  95.2 15.3 %wo.4 = (bf16[512,2560]{1,0:T(8,128)(2,1)}, bf16[512,2560]{1,0:T(8,128)(2,1)}) custom-call(s32[2]{0:T(128)} %pad_add_fusion.at_ref, bf16[1024,2560]{1,0:T(8,128)(2,1)} %x_ref.5, bf16[512,1024]{1,0:T(8,128)(2,1)} %window.2.o0_ref, bf16[512,1024]{1,0:T(8,128)(2,1)} %collective-permute-done.4.o1_ref, bf16[2,1024,2560]{2,1,0:T(8,128)(2,1)} %w_ref.7, ...), custom_call_target="tpu_custom_call" | custom-call | flops 5368709120 | bytes 18350080 | tf_op jit(solution)/shard_map/wo/pallas_call | solution.py:414
  110.5 50.4 %ffn.4.d0_ref = bf16[512,2560]{1,0:T(8,128)(2,1)} custom-call(bf16[512,2560]{1,0:T(8,128)(2,1)} %get-tuple-element.68.u_ref, bf16[2,2560,5120]{2,1,0:T(8,128)(2,1)} %wg_ref.7, bf16[2,2560,5120]{2,1,0:T(8,128)(2,1)} %wu_ref.7, bf16[2,5120,2560]{2,1,0:T(8,128)(2,1)} %wd_ref.7), custom_call_target="tpu_custom_call" | custom-call | flops 40265318400 | bytes 83886080 | tf_op jit(solution)/shard_map/ffn/pallas_call | solution.py:455
  161.5 15.3 %wo.5 = (bf16[512,2560]{1,0:T(8,128)(2,1)}, bf16[512,2560]{1,0:T(8,128)(2,1)}) custom-call(s32[2]{0:T(128)} %pad_add_fusion.at_ref, bf16[1024,2560]{1,0:T(8,128)(2,1)} %x_ref.5, bf16[512,1024]{1,0:T(8,128)(2,1)} %window.3.o0_ref, bf16[512,1024]{1,0:T(8,128)(2,1)} %collective-permute-done.8.o1_ref, bf16[2,1024,2560]{2,1,0:T(8,128)(2,1)} %w_ref.7, ...), custom_call_target="tpu_custom_call" | custom-call | flops 5368709120 | bytes 18350080 | tf_op jit(solution)/shard_map/wo/pallas_call | solution.py:414
  176.7 49.9 %ffn.5.d0_ref = bf16[512,2560]{1,0:T(8,128)(2,1)} custom-call(bf16[512,2560]{1,0:T(8,128)(2,1)} %get-tuple-element.74.u_ref, bf16[2,2560,5120]{2,1,0:T(8,128)(2,1)} %wg_ref.7, bf16[2,2560,5120]{2,1,0:T(8,128)(2,1)} %wu_ref.7, bf16[2,5120,2560]{2,1,0:T(8,128)(2,1)} %wd_ref.7), custom_call_target="tpu_custom_call" | custom-call | flops 40265318400 | bytes 83886080 | tf_op jit(solution)/shard_map/ffn/pallas_call | solution.py:455
  228.2 15.5 %qkv.2 = (bf16[4,512,256]{2,1,0:T(8,128)(2,1)}, bf16[512,512]{1,0:T(8,128)(2,1)}, bf16[512,512]{1,0:T(8,128)(2,1)}, bf16[512,2560]{1,0:T(8,128)(2,1)}) custom-call(bf16[512,2560]{1,0:T(8,128)(2,1)} %get-tuple-element.67.x_ref, bf16[512,2560]{1,0:T(8,128)(2,1)} %ffn.4.d0_ref, bf16[512,2560]{1,0:T(8,128)(2,1)} %collective-permute-done.7.d1_ref, ...), custom_call_target="tpu_custom_call" | custom-call | flops 5368709120 | bytes 15204352 | tf_op jit(solution)/shard_map/qkv/pallas_call | solution.py:63
  243.7 12.8 %multiply_reduce_fusion = f32[6144,2]{1,0:T(8,128)S(1)} fusion(bf16[6144,2,256]{2,1,0:T(2,128)(2,1)} %param.21), kind=kLoop, calls=%fused_computation | loop fusion | flops 9424896 | bytes 6340608 | tf_op jit(solution)/shard_map/reduce_sum | solution.py:564
  270.0 23.8 %gattn.8 = (bf16[512,1024]{1,0:T(8,128)(2,1)}, bf16[512,128]{1,0:T(8,128)(2,1)}) custom-call(s32[2]{0:T(128)} %pad_add_fusion.2.refs_0_, f32[2]{0:T(128)} %sqrt.9.refs_1_, bf16[4,512,256]{2,1,0:T(8,128)(2,1)} %collective-permute-done.9.refs_2_, bf16[6144,512]{1,0:T(8,128)(2,1)} %bitcast.51, bf16[6144,512]{1,0:T(8,128)(2,1)} %bitcast.58), custom_call_target="tpu_custom_call" | custom-call | flops 12884901888 | bytes 14680064 | tf_op jit(solution)/shard_map/gattn/pallas_call | solution.py:375
  293.9 15.6 %qkv.3 = (bf16[4,512,256]{2,1,0:T(8,128)(2,1)}, bf16[512,512]{1,0:T(8,128)(2,1)}, bf16[512,512]{1,0:T(8,128)(2,1)}, bf16[512,2560]{1,0:T(8,128)(2,1)}) custom-call(bf16[512,2560]{1,0:T(8,128)(2,1)} %get-tuple-element.73.x_ref, bf16[512,2560]{1,0:T(8,128)(2,1)} %ffn.5.d0_ref, bf16[512,2560]{1,0:T(8,128)(2,1)} %collective-permute-done.11.d1_ref, ...), custom_call_target="tpu_custom_call" | custom-call | flops 5368709120 | bytes 15204352 | tf_op jit(solution)/shard_map/qkv/pallas_call | solution.py:63
  315.5 27.0 %gattn.9 = (bf16[512,1024]{1,0:T(8,128)(2,1)}, bf16[512,128]{1,0:T(8,128)(2,1)}) custom-call(s32[2]{0:T(128)} %pad_add_fusion.2.refs_0_, f32[2]{0:T(128)} %sqrt_maximum_fusion.refs_1_, bf16[4,512,256]{2,1,0:T(8,128)(2,1)} %collective-permute-done.14.refs_2_, bf16[6144,512]{1,0:T(8,128)(2,1)} %bitcast.52, bf16[6144,512]{1,0:T(8,128)(2,1)} %bitcast.59, ...), custom_call_target="tpu_custom_call" | custom-call | flops 15032385536 | bytes 16777216 | tf_op jit(solution)/shard_map/gattn/pallas_call | solution.py:375
  342.5 44.9 %gattn.10 = (bf16[512,1024]{1,0:T(8,128)(2,1)}, bf16[512,128]{1,0:T(8,128)(2,1)}, bf16[512,1024]{1,0:T(8,128)(2,1)}, bf16[512,128]{1,0:T(8,128)(2,1)}) custom-call(s32[2]{0:T(128)} %pad_add_fusion.4.refs_0_, f32[2]{0:T(128)} %sqrt_maximum_fusion.refs_1_, bf16[4,512,256]{2,1,0:T(8,128)(2,1)} %collective-permute-done.13.refs_2_, ...), custom_call_target="tpu_custom_call" | custom-call | flops 30064771072 | bytes 18874368 | tf_op jit(solution)/shard_map/gattn/pallas_call | solution.py:375
  393.3 9.6 %gattn.11 = (bf16[512,1024]{1,0:T(8,128)(2,1)}, bf16[512,128]{1,0:T(8,128)(2,1)}) custom-call(s32[2]{0:T(128)} %pad_add_fusion.2.refs_0_, f32[2]{0:T(128)} %sqrt_maximum_fusion.refs_1_, bf16[4,512,256]{2,1,0:T(8,128)(2,1)} %collective-permute-done.9.refs_2_, bf16[512,512]{1,0:T(8,128)(2,1)} %get-tuple-element.75.refs_5_.refs_6_.refs_3_, ...), custom_call_target="tpu_custom_call" | custom-call | flops 2147483648 | bytes 4194304 | tf_op jit(solution)/shard_map/gattn/pallas_call | solution.py:375
  404.0 29.2 %gattn.12 = (bf16[512,1024]{1,0:T(8,128)(2,1)}, bf16[512,128]{1,0:T(8,128)(2,1)}) custom-call(s32[2]{0:T(128)} %pad_add_fusion.3.refs_0_, f32[2]{0:T(128)} %sqrt_maximum_fusion.refs_1_, bf16[4,512,256]{2,1,0:T(8,128)(2,1)} %collective-permute-done.15.refs_2_, bf16[6144,512]{1,0:T(8,128)(2,1)} %bitcast.54, bf16[6144,512]{1,0:T(8,128)(2,1)} %bitcast.61, ...), custom_call_target="tpu_custom_call" | custom-call | flops 15032385536 | bytes 16777216 | tf_op jit(solution)/shard_map/gattn/pallas_call | solution.py:375
  435.1 29.3 %gattn.13 = (bf16[512,1024]{1,0:T(8,128)(2,1)}, bf16[512,128]{1,0:T(8,128)(2,1)}) custom-call(s32[2]{0:T(128)} %pad_add_fusion.3.refs_0_, f32[2]{0:T(128)} %sqrt_maximum_fusion.refs_1_, bf16[4,512,256]{2,1,0:T(8,128)(2,1)} %collective-permute-done.12.refs_2_, bf16[6144,512]{1,0:T(8,128)(2,1)} %bitcast.55, bf16[6144,512]{1,0:T(8,128)(2,1)} %bitcast.62, ...), custom_call_target="tpu_custom_call" | custom-call | flops 15032385536 | bytes 16777216 | tf_op jit(solution)/shard_map/gattn/pallas_call | solution.py:375
  467.1 29.0 %gattn.14.o0_ref = bf16[512,1024]{1,0:T(8,128)(2,1)} custom-call(s32[2]{0:T(128)} %pad_add_fusion.1.refs_0_, f32[2]{0:T(128)} %sqrt_maximum_fusion.refs_1_, bf16[4,512,256]{2,1,0:T(8,128)(2,1)} %get-tuple-element.93.refs_2_, bf16[6144,512]{1,0:T(8,128)(2,1)} %bitcast.56, bf16[6144,512]{1,0:T(8,128)(2,1)} %bitcast.63, ...), custom_call_target="tpu_custom_call" | custom-call | flops 15032385536 | bytes 16777216 | tf_op jit(solution)/shard_map/gattn/pallas_call | solution.py:375
  498.4 29.9 %gattn.15.o0_ref = bf16[512,1024]{1,0:T(8,128)(2,1)} custom-call(s32[2]{0:T(128)} %pad_add_fusion.1.refs_0_, f32[2]{0:T(128)} %sqrt_maximum_fusion.refs_1_, bf16[4,512,256]{2,1,0:T(8,128)(2,1)} %get-tuple-element.96.refs_2_, bf16[6144,512]{1,0:T(8,128)(2,1)} %bitcast.57, bf16[6144,512]{1,0:T(8,128)(2,1)} %bitcast.64, ...), custom_call_target="tpu_custom_call" | custom-call | flops 15032385536 | bytes 16777216 | tf_op jit(solution)/shard_map/gattn/pallas_call | solution.py:375
  528.8 15.5 %wo.7 = (bf16[512,2560]{1,0:T(8,128)(2,1)}, bf16[512,2560]{1,0:T(8,128)(2,1)}) custom-call(s32[2]{0:T(128)} %pad_add_fusion.at_ref, bf16[512,2560]{1,0:T(8,128)(2,1)} %get-tuple-element.103.x_ref, bf16[512,1024]{1,0:T(8,128)(2,1)} %gattn.14.o0_ref, bf16[512,1024]{1,0:T(8,128)(2,1)} %collective-permute-done.32.o1_ref, bf16[2,1024,2560]{2,1,0:T(8,128)(2,1)} %w_ref.7, ...), custom_call_target="tpu_custom_call" | custom-call | flops 5368709120 | bytes 18350080 | tf_op jit(solution)/shard_map/wo/pallas_call | solution.py:414
  544.3 49.8 %ffn.7.d0_ref = bf16[512,2560]{1,0:T(8,128)(2,1)} custom-call(bf16[512,2560]{1,0:T(8,128)(2,1)} %get-tuple-element.105.u_ref, bf16[2,2560,5120]{2,1,0:T(8,128)(2,1)} %wg_ref.7, bf16[2,2560,5120]{2,1,0:T(8,128)(2,1)} %wu_ref.7, bf16[2,5120,2560]{2,1,0:T(8,128)(2,1)} %wd_ref.7), custom_call_target="tpu_custom_call" | custom-call | flops 40265318400 | bytes 83886080 | tf_op jit(solution)/shard_map/ffn/pallas_call | solution.py:455
  595.6 15.7 %wo.6 = (bf16[512,2560]{1,0:T(8,128)(2,1)}, bf16[512,2560]{1,0:T(8,128)(2,1)}) custom-call(s32[2]{0:T(128)} %pad_add_fusion.at_ref, bf16[512,2560]{1,0:T(8,128)(2,1)} %get-tuple-element.69.x_ref, bf16[512,1024]{1,0:T(8,128)(2,1)} %gattn.15.o0_ref, bf16[512,1024]{1,0:T(8,128)(2,1)} %collective-permute-done.28.o1_ref, bf16[2,1024,2560]{2,1,0:T(8,128)(2,1)} %w_ref.7, ...), custom_call_target="tpu_custom_call" | custom-call | flops 5368709120 | bytes 18350080 | tf_op jit(solution)/shard_map/wo/pallas_call | solution.py:414
  611.3 49.9 %ffn.6.d0_ref = bf16[512,2560]{1,0:T(8,128)(2,1)} custom-call(bf16[512,2560]{1,0:T(8,128)(2,1)} %get-tuple-element.102.u_ref, bf16[2,2560,5120]{2,1,0:T(8,128)(2,1)} %wg_ref.7, bf16[2,2560,5120]{2,1,0:T(8,128)(2,1)} %wu_ref.7, bf16[2,5120,2560]{2,1,0:T(8,128)(2,1)} %wd_ref.7), custom_call_target="tpu_custom_call" | custom-call | flops 40265318400 | bytes 83886080 | tf_op jit(solution)/shard_map/ffn/pallas_call | solution.py:455
  673.7 45.5 %collective-permute-done.31.d1_ref = bf16[512,2560]{1,0:T(8,128)(2,1)} collective-permute-done((bf16[512,2560]{1,0:T(8,128)(2,1)}, bf16[512,2560]{1,0:T(8,128)(2,1)}, u32[]{:S(2)}, u32[]{:S(2)}) %collective-permute-start.31) | collective-permute-done | bytes 2621472 | tf_op jit(solution)/shard_map/ppermute | solution.py:520
  (156 shorter events, 96.7 us)
Async XLA Ops:
  4.2 65.0 %collective-permute-start.5 = (bf16[512,2560]{1,0:T(8,128)(2,1)}, bf16[512,2560]{1,0:T(8,128)(2,1)}, u32[]{:S(2)}, u32[]{:S(2)}) collective-permute-start(bf16[512,2560]{1,0:T(8,128)(2,1)} %dynamic-slice_bitcast_fusion.1), channel_id=1, source_target_pairs={{0,4},{4,0},{1,5},{5,1},{2,6},{6,2},{3,7},{7,3}} | collective-permute-start | bytes 7864328 | tf_op jit(solution)/shard_map/ppermute | solution.py:520
  25.0 27.4 %collective-permute-start = (bf16[512,512]{1,0:T(8,128)(2,1)}, bf16[512,512]{1,0:T(8,128)(2,1)}, u32[]{:S(2)}, u32[]{:S(2)}) collective-permute-start(bf16[512,512]{1,0:T(8,128)(2,1)} %get-tuple-element.57.refs_5_.refs_9_), channel_id=1, source_target_pairs={{0,1},{1,2},{2,3},{4,5},{5,6},{6,7}} | collective-permute-start | bytes 1572872 | tf_op jit(solution)/shard_map/ppermute | solution.py:540
  73.5 88.0 %collective-permute-start.8 = (bf16[512,1024]{1,0:T(8,128)(2,1)}, bf16[512,1024]{1,0:T(8,128)(2,1)}, u32[]{:S(2)}, u32[]{:S(2)}) collective-permute-start(bf16[512,1024]{1,0:T(8,128)(2,1)} %window.3.o0_ref), channel_id=1, source_target_pairs={{0,4},{4,0},{1,5},{5,1},{2,6},{6,2},{3,7},{7,3}} | collective-permute-start | bytes 3145736 | tf_op jit(solution)/shard_map/ppermute | solution.py:520
  161.0 67.2 %collective-permute-start.7 = (bf16[512,2560]{1,0:T(8,128)(2,1)}, bf16[512,2560]{1,0:T(8,128)(2,1)}, u32[]{:S(2)}, u32[]{:S(2)}) collective-permute-start(bf16[512,2560]{1,0:T(8,128)(2,1)} %ffn.4.d0_ref), channel_id=1, source_target_pairs={{0,4},{4,0},{1,5},{5,1},{2,6},{6,2},{3,7},{7,3}} | collective-permute-start | bytes 7864328 | tf_op jit(solution)/shard_map/ppermute | solution.py:520
  226.6 67.3 %collective-permute-start.11 = (bf16[512,2560]{1,0:T(8,128)(2,1)}, bf16[512,2560]{1,0:T(8,128)(2,1)}, u32[]{:S(2)}, u32[]{:S(2)}) collective-permute-start(bf16[512,2560]{1,0:T(8,128)(2,1)} %ffn.5.d0_ref), channel_id=1, source_target_pairs={{0,4},{4,0},{1,5},{5,1},{2,6},{6,2},{3,7},{7,3}} | collective-permute-start | bytes 7864328 | tf_op jit(solution)/shard_map/ppermute | solution.py:520
  311.8 30.7 %collective-permute-start.13 = (bf16[4,512,256]{2,1,0:T(8,128)(2,1)}, bf16[4,512,256]{2,1,0:T(8,128)(2,1)}, u32[]{:S(2)}, u32[]{:S(2)}) collective-permute-start(bf16[4,512,256]{2,1,0:T(8,128)(2,1)} %get-tuple-element.93.refs_2_), channel_id=1, source_target_pairs={{0,2},{1,3},{2,0},{3,1},{4,6},{5,7},{6,4},{7,5}} | collective-permute-start | bytes 3145736 | tf_op jit(solution)/shard_map/ppermute | solution.py:519
  342.5 60.4 %collective-permute-start.15 = (bf16[4,512,256]{2,1,0:T(8,128)(2,1)}, bf16[4,512,256]{2,1,0:T(8,128)(2,1)}, u32[]{:S(2)}, u32[]{:S(2)}) collective-permute-start(bf16[4,512,256]{2,1,0:T(8,128)(2,1)} %collective-permute-done.13.refs_2_), channel_id=1, source_target_pairs={{0,1},{1,0},{2,3},{3,2},{4,5},{5,4},{6,7},{7,6}} | collective-permute-start | bytes 3145736 | tf_op jit(solution)/shard_map/ppermute | solution.py:519
  389.2 43.9 %collective-permute-start.12 = (bf16[4,512,256]{2,1,0:T(8,128)(2,1)}, bf16[4,512,256]{2,1,0:T(8,128)(2,1)}, u32[]{:S(2)}, u32[]{:S(2)}) collective-permute-start(bf16[4,512,256]{2,1,0:T(8,128)(2,1)} %collective-permute-done.10.refs_3_), channel_id=1, source_target_pairs={{0,1},{1,0},{2,3},{3,2},{4,5},{5,4},{6,7},{7,6}} | collective-permute-start | bytes 3145736 | tf_op jit(solution)/shard_map/ppermute | solution.py:519
  389.3 75.7 %collective-permute-start.20 = (bf16[512,1024]{1,0:T(8,128)(2,1)}, bf16[512,1024]{1,0:T(8,128)(2,1)}, u32[]{:S(2)}, u32[]{:S(2)}) collective-permute-start(bf16[512,1024]{1,0:T(8,128)(2,1)} %get-tuple-element.80), channel_id=1, source_target_pairs={{0,1},{1,0},{2,3},{3,2},{4,5},{5,4},{6,7},{7,6}} | collective-permute-start | bytes 3145736 | tf_op jit(solution)/shard_map/ppermute | solution.py:519
  402.9 30.4 %collective-permute-start.18 = (bf16[512,1024]{1,0:T(8,128)(2,1)}, bf16[512,1024]{1,0:T(8,128)(2,1)}, u32[]{:S(2)}, u32[]{:S(2)}) collective-permute-start(bf16[512,1024]{1,0:T(8,128)(2,1)} %get-tuple-element.90), channel_id=1, source_target_pairs={{0,1},{1,0},{2,3},{3,2},{4,5},{5,4},{6,7},{7,6}} | collective-permute-start | bytes 3145736 | tf_op jit(solution)/shard_map/ppermute | solution.py:519
  403.0 30.3 %collective-permute-start.19 = (bf16[512,128]{1,0:T(8,128)(2,1)S(1)}, bf16[512,128]{1,0:T(8,128)(2,1)S(1)}, u32[]{:S(2)}, u32[]{:S(2)}) collective-permute-start(bf16[512,128]{1,0:T(8,128)(2,1)S(1)} %copy-done.12), channel_id=1, source_target_pairs={{0,1},{1,0},{2,3},{3,2},{4,5},{5,4},{6,7},{7,6}} | collective-permute-start | bytes 393224 | tf_op jit(solution)/shard_map/ppermute | solution.py:519
  403.5 60.9 %collective-permute-start.29 = (bf16[512,2560]{1,0:T(8,128)(2,1)}, bf16[512,2560]{1,0:T(8,128)(2,1)}, u32[]{:S(2)}, u32[]{:S(2)}) collective-permute-start(bf16[512,2560]{1,0:T(8,128)(2,1)} %dynamic-slice_bitcast_fusion), channel_id=1, source_target_pairs={{0,4},{4,0},{1,5},{5,1},{2,6},{6,2},{3,7},{7,3}} | collective-permute-start | bytes 7864328 | tf_op jit(solution)/shard_map/ppermute | solution.py:520
  433.1 31.7 %collective-permute-start.21 = (bf16[512,128]{1,0:T(8,128)(2,1)S(1)}, bf16[512,128]{1,0:T(8,128)(2,1)S(1)}, u32[]{:S(2)}, u32[]{:S(2)}) collective-permute-start(bf16[512,128]{1,0:T(8,128)(2,1)S(1)} %copy-done.10), channel_id=1, source_target_pairs={{0,1},{1,0},{2,3},{3,2},{4,5},{5,4},{6,7},{7,6}} | collective-permute-start | bytes 393224 | tf_op jit(solution)/shard_map/ppermute | solution.py:519
  433.3 33.4 %collective-permute-start.22 = (bf16[512,1024]{1,0:T(8,128)(2,1)}, bf16[512,1024]{1,0:T(8,128)(2,1)}, u32[]{:S(2)}, u32[]{:S(2)}) collective-permute-start(bf16[512,1024]{1,0:T(8,128)(2,1)} %get-tuple-element.88), channel_id=1, source_target_pairs={{0,3},{1,2},{2,1},{3,0},{4,7},{5,6},{6,5},{7,4}} | collective-permute-start | bytes 3145736 | tf_op jit(solution)/shard_map/ppermute | solution.py:519
  433.3 31.6 %collective-permute-start.23 = (bf16[512,128]{1,0:T(8,128)(2,1)}, bf16[512,128]{1,0:T(8,128)(2,1)S(1)}, u32[]{:S(2)}, u32[]{:S(2)}) collective-permute-start(bf16[512,128]{1,0:T(8,128)(2,1)} %get-tuple-element.95), channel_id=1, source_target_pairs={{0,3},{1,2},{2,1},{3,0},{4,7},{5,6},{6,5},{7,4}} | collective-permute-start | bytes 393224 | tf_op jit(solution)/shard_map/ppermute | solution.py:519
  464.4 33.3 %collective-permute-start.24 = (bf16[512,1024]{1,0:T(8,128)(2,1)}, bf16[512,1024]{1,0:T(8,128)(2,1)}, u32[]{:S(2)}, u32[]{:S(2)}) collective-permute-start(bf16[512,1024]{1,0:T(8,128)(2,1)} %get-tuple-element.85), channel_id=1, source_target_pairs={{0,1},{1,0},{2,3},{3,2},{4,5},{5,4},{6,7},{7,6}} | collective-permute-start | bytes 3145736 | tf_op jit(solution)/shard_map/ppermute | solution.py:519
  464.8 31.3 %collective-permute-start.25 = (bf16[512,128]{1,0:T(8,128)(2,1)S(1)}, bf16[512,128]{1,0:T(8,128)(2,1)S(1)}, u32[]{:S(2)}, u32[]{:S(2)}) collective-permute-start(bf16[512,128]{1,0:T(8,128)(2,1)S(1)} %copy-done.11), channel_id=1, source_target_pairs={{0,1},{1,0},{2,3},{3,2},{4,5},{5,4},{6,7},{7,6}} | collective-permute-start | bytes 393224 | tf_op jit(solution)/shard_map/ppermute | solution.py:519
  465.0 32.8 %collective-permute-start.26 = (bf16[512,1024]{1,0:T(8,128)(2,1)}, bf16[512,1024]{1,0:T(8,128)(2,1)}, u32[]{:S(2)}, u32[]{:S(2)}) collective-permute-start(bf16[512,1024]{1,0:T(8,128)(2,1)} %get-tuple-element.92), channel_id=1, source_target_pairs={{0,3},{1,2},{2,1},{3,0},{4,7},{5,6},{6,5},{7,4}} | collective-permute-start | bytes 3145736 | tf_op jit(solution)/shard_map/ppermute | solution.py:519
  465.0 32.7 %collective-permute-start.27 = (bf16[512,128]{1,0:T(8,128)(2,1)}, bf16[512,128]{1,0:T(8,128)(2,1)S(1)}, u32[]{:S(2)}, u32[]{:S(2)}) collective-permute-start(bf16[512,128]{1,0:T(8,128)(2,1)} %get-tuple-element.98), channel_id=1, source_target_pairs={{0,3},{1,2},{2,1},{3,0},{4,7},{5,6},{6,5},{7,4}} | collective-permute-start | bytes 393224 | tf_op jit(solution)/shard_map/ppermute | solution.py:519
  466.7 62.1 %collective-permute-start.30 = (bf16[512,2560]{1,0:T(8,128)(2,1)}, bf16[512,2560]{1,0:T(8,128)(2,1)}, u32[]{:S(2)}, u32[]{:S(2)}) collective-permute-start(bf16[512,2560]{1,0:T(8,128)(2,1)} %collective-permute-done.29.near_ref), channel_id=1, source_target_pairs={{0,1},{1,0},{2,3},{3,2},{4,5},{5,4},{6,7},{7,6}} | collective-permute-start | bytes 7864328 | tf_op jit(solution)/shard_map/ppermute | solution.py:519
  496.1 32.6 %collective-permute-start.32 = (bf16[512,1024]{1,0:T(8,128)(2,1)}, bf16[512,1024]{1,0:T(8,128)(2,1)}, u32[]{:S(2)}, u32[]{:S(2)}) collective-permute-start(bf16[512,1024]{1,0:T(8,128)(2,1)} %gattn.14.o0_ref), channel_id=1, source_target_pairs={{0,4},{4,0},{1,5},{5,1},{2,6},{6,2},{3,7},{7,3}} | collective-permute-start | bytes 3145736 | tf_op jit(solution)/shard_map/ppermute | solution.py:520
  528.3 67.3 %collective-permute-start.28 = (bf16[512,1024]{1,0:T(8,128)(2,1)}, bf16[512,1024]{1,0:T(8,128)(2,1)}, u32[]{:S(2)}, u32[]{:S(2)}) collective-permute-start(bf16[512,1024]{1,0:T(8,128)(2,1)} %gattn.15.o0_ref), channel_id=1, source_target_pairs={{0,4},{4,0},{1,5},{5,1},{2,6},{6,2},{3,7},{7,3}} | collective-permute-start | bytes 3145736 | tf_op jit(solution)/shard_map/ppermute | solution.py:520
  594.1 74.0 %collective-permute-start.33 = (bf16[512,2560]{1,0:T(8,128)(2,1)}, bf16[512,2560]{1,0:T(8,128)(2,1)}, u32[]{:S(2)}, u32[]{:S(2)}) collective-permute-start(bf16[512,2560]{1,0:T(8,128)(2,1)} %ffn.7.d0_ref), channel_id=1, source_target_pairs={{0,4},{4,0},{1,5},{5,1},{2,6},{6,2},{3,7},{7,3}} | collective-permute-start | bytes 7864328 | tf_op jit(solution)/shard_map/ppermute | solution.py:520
  661.2 58.0 %collective-permute-start.31 = (bf16[512,2560]{1,0:T(8,128)(2,1)}, bf16[512,2560]{1,0:T(8,128)(2,1)}, u32[]{:S(2)}, u32[]{:S(2)}) collective-permute-start(bf16[512,2560]{1,0:T(8,128)(2,1)} %ffn.6.d0_ref), channel_id=1, source_target_pairs={{0,4},{4,0},{1,5},{5,1},{2,6},{6,2},{3,7},{7,3}} | collective-permute-start | bytes 7864328 | tf_op jit(solution)/shard_map/ppermute | solution.py:520
  (33 other events, 453.2 us)
